TPU v7x, 256 devices: a whole 4x4x8 slice. The times are simulated.
256 devices in a mesh: slab: 8 (over y, core), bl: 32 (over z, x).
Axes of the slice: x: 4, y: 4, z: 8, core: 2. Of those that a mesh axis runs over, the one named last changes fastest.
Arguments:
- model_image: float32 [2, 8192, 8192], P(None, 'slab', 'bl'), may hold values from -6 to 6
- vis_coords: float32 [4096, 2, 128], P(('slab', 'bl')), may hold values from 0 to 32
- vis_observed: float32 [4096, 2, 128], P(('slab', 'bl')), may hold values from -6 to 6
- tile_slot: int32 [4096], P(('slab', 'bl')), may hold values from 0 to 255
- tile_group: int32 [4096, 1], P(('slab', 'bl')), may hold values from 0 to 31; in each aligned block of 16 rows (0 to 15, 16 to 31, ...) at most 2 rows name the same one
- w_plane: int32 [4096], P(('slab', 'bl')), may hold values from 0 to 7
- vis_count: int32 [4096], P(('slab', 'bl')), may hold values from 16 to 128, as said below
Outputs:
- residual_image: float32 [2, 8192, 8192], P(None, 'slab', 'bl')
- residual_vis: float32 [4096, 2, 128], P(('slab', 'bl'))
Inputs may be any that keep to these rules, and one draw needn't show every extreme that they name: `tile_group`: among the 16 subgrids of one device, at most 2 name the same group. `vis_count`: some subgrid holds exactly 128 visibilities.
All inputs are finite; a program needn't handle non-finite values.
Results may differ from a plain program's by a relative error of at most 0.0003.
Values sent between devices are 32-bit elements; how exact they have to be, the bound alone decides.
A program may use at most 128 MiB of HBM per device.

v0:
```python
import math

import jax
import jax.numpy as jnp
from jax import lax
from jax.sharding import Mesh
from jax.sharding import PartitionSpec as P

N = 8192
SUB = 32
FA = 128
BL = ("bl_0", "bl_1")
SLAB_BL = ("slab", "bl_0", "bl_1")


w_step = 0.1


def in_blocks(value, dim, count):
    before, after = (value.shape[:dim], value.shape[dim + 1 :])
    return jnp.moveaxis(value.reshape(*before, count, -1, *after), dim, 0)


def laid_out(parts, dim):
    shape = list(parts.shape[1:])
    shape[dim] *= parts.shape[0]
    return jnp.moveaxis(parts, 0, dim).reshape(shape)


def joined_exchange(value, axis, axes, splits, concats):
    sizes = [lax.axis_size(a) for a in axes]
    parts = in_blocks(value, splits[0], sizes[0])
    parts = jnp.moveaxis(in_blocks(parts, splits[1] + 1, sizes[1]), 0, 1)
    inside = parts.shape[2:]
    parts = parts.reshape(-1, *inside)
    parts = lax.all_to_all(parts, axis, split_axis=0, concat_axis=0, tiled=True)
    parts = laid_out(parts.reshape(*sizes, *inside), concats[0] + 1)
    return laid_out(parts, concats[1])


def exchange_in_order(parts, axes, order):
    shape = [lax.axis_size(a) for a in axes]
    parts = parts.reshape(*shape, *parts.shape[1:])
    for k in order:
        parts = lax.all_to_all(parts, axes[k], split_axis=k, concat_axis=k, tiled=True)
    return parts.reshape(-1, *parts.shape[len(axes) :])


def exchange_by_axis(value, axes, order, split_dim, concat_dim):
    parts = in_blocks(value, split_dim, lax.axis_size(axes))
    return laid_out(exchange_in_order(parts, axes, order), concat_dim)


def piece_ends(length, count):
    unit = 8 if length >= 8 * count else 1
    return [length // unit * k // count * unit for k in range(1, count)]


def several_exchanges(value, axis, pieces, split_dim, concat_dim):
    parts = in_blocks(value, split_dim, lax.axis_size(axis))
    cut = max(range(1, max(2, parts.ndim - 1)), key=lambda d: parts.shape[d])
    gathered = []
    for section in jnp.split(parts, piece_ends(parts.shape[cut], pieces), axis=cut):
        if section.size:
            gathered.append(lax.all_to_all(section, axis, split_axis=0, concat_axis=0, tiled=True))
    return laid_out(jnp.concatenate(gathered, axis=cut), concat_dim)


def complex_einsum(form, left, right):
    product = lambda first, second: jnp.einsum(form, first, second, precision=lax.Precision.HIGHEST)
    return (
        product(left[0], right[0]) - product(left[1], right[1]),
        product(left[0], right[1]) + product(left[1], right[0]),
    )


def complex_mul(left, right):
    return (left[0] * right[0] - left[1] * right[1], left[0] * right[1] + left[1] * right[0])


def subgrid_pass(tile_real, tile_imag, coords, observed, planes, counts):
    width = tile_real.shape[-1]
    half = width // 2
    slots = coords.shape[-1]
    index = jnp.arange(width, dtype=jnp.int32)
    offsets = (index - half).astype(jnp.float32)
    turns = index[:, None] * (index[None, :] - half) % width
    angle = 2.0 * math.pi / width * turns.astype(jnp.float32)
    forward_d = (jnp.cos(angle), jnp.sin(angle))
    backward_d = (forward_d[0], -forward_d[1])
    scale_sub = 1.0 / (width * width)
    halfway = complex_einsum("il,kij->klj", forward_d, (tile_real, tile_imag))
    image_sub = complex_einsum("klj,jm->klm", halfway, forward_d)
    image_sub = (image_sub[0] * scale_sub, image_sub[1] * scale_sub)
    radius = (offsets[:, None] ** 2 + offsets[None, :] ** 2) / (half * half)
    phase = -w_step * planes.astype(jnp.float32)[:, None, None] * radius[None]
    screen = (jnp.cos(phase), jnp.sin(phase))
    weighted = complex_mul(screen, image_sub)
    along_a = -2.0 * math.pi / width * coords[:, 0, :][:, None, :] * offsets[None, :, None]
    along_b = -2.0 * math.pi / width * coords[:, 1, :][:, None, :] * offsets[None, :, None]
    phase_a = (jnp.cos(along_a), jnp.sin(along_a))
    phase_b = (jnp.cos(along_b), jnp.sin(along_b))
    partial_rows = complex_einsum("klm,kmj->klj", weighted, phase_b)
    terms = complex_mul(phase_a, partial_rows)
    predicted = (jnp.sum(terms[0], axis=1), jnp.sum(terms[1], axis=1))
    live = (jnp.arange(slots, dtype=jnp.int32)[None, :] < counts[:, None]).astype(jnp.float32)
    resid_real = (observed[:, 0, :] - predicted[0]) * live
    resid_imag = (observed[:, 1, :] - predicted[1]) * live
    spread = complex_mul(
        (phase_a[0], -phase_a[1]), (resid_real[:, None, :], resid_imag[:, None, :])
    )
    collected = complex_einsum("klj,kmj->klm", spread, (phase_b[0], -phase_b[1]))
    unscreened = complex_mul((screen[0], -screen[1]), collected)
    middle = complex_einsum("il,klm->kim", backward_d, unscreened)
    tile_out = complex_einsum("kim,jm->kij", middle, backward_d)
    return (
        jnp.stack([resid_real, resid_imag], axis=1),
        jnp.stack([tile_out[0] * scale_sub, tile_out[1] * scale_sub], axis=1),
    )


def run_blocks(tile_stack, coords, observed, planes, counts):
    total = tile_stack.shape[0]
    slots = coords.shape[-1]
    width = tile_stack.shape[-1]
    block_size = math.gcd(total, 64)
    block_count = total // block_size

    def one_block(pieces):
        block_tiles, block_coords, block_obs, block_planes, block_counts = pieces
        return subgrid_pass(
            block_tiles[:, 0],
            block_tiles[:, 1],
            block_coords,
            block_obs,
            block_planes,
            block_counts,
        )

    resid_vis, contrib = lax.map(
        one_block,
        (
            tile_stack.reshape(block_count, block_size, 2, width, width),
            coords.reshape(block_count, block_size, 2, slots),
            observed.reshape(block_count, block_size, 2, slots),
            planes.reshape(block_count, block_size),
            counts.reshape(block_count, block_size),
        ),
    )
    return (resid_vis.reshape(total, 2, slots), contrib.reshape(total, 2 * width * width))


def dft_table(rows_count, cols_count, modulus, turn_sign):
    product = (
        lax.broadcasted_iota(jnp.int32, (rows_count, cols_count), 0)
        * lax.broadcasted_iota(jnp.int32, (rows_count, cols_count), 1)
        % modulus
    )
    angle = 2.0 * math.pi / modulus * product.astype(jnp.float32)
    return (jnp.cos(angle), turn_sign * jnp.sin(angle))


def dft_last(real_part, imag_part, turn_sign):
    length = real_part.shape[-1]
    inner = FA
    outer = length // inner
    leading = real_part.shape[:-1]
    outer_table = dft_table(outer, outer, outer, turn_sign)
    twiddle = dft_table(outer, inner, length, turn_sign)
    inner_table = dft_table(inner, inner, inner, turn_sign)
    shaped = (
        real_part.reshape(leading + (outer, inner)),
        imag_part.reshape(leading + (outer, inner)),
    )
    first_pass = complex_einsum("...ca,vc->...va", shaped, outer_table)
    first_pass = complex_mul(first_pass, twiddle)
    second_pass = complex_einsum("...va,wa->...wv", first_pass, inner_table)
    return (
        second_pass[0].reshape(leading + (length,)),
        second_pass[1].reshape(leading + (length,)),
    )


def to_columns(block):
    groups = lax.axis_size(BL)
    bands = lax.axis_size("slab")
    depth = block.shape[1]
    peers = block.shape[2] // depth
    packed = (
        block.reshape(2, depth, peers, depth)
        .transpose(0, 2, 1, 3)
        .reshape(2, 1, peers, depth * depth)
    )
    moved = joined_exchange(packed, SLAB_BL, ("slab", BL), (2, 2), (1, 1))
    shaped = moved.reshape(2, groups, bands, depth, depth)
    return shaped.transpose(0, 4, 2, 1, 3).reshape(2, depth, groups * bands * depth)


def per_device(model_image, vis_coords, vis_observed, tile_slot, tile_group, w_plane, vis_count):
    groups = lax.axis_size(BL)
    spread_rows = lax.all_to_all(model_image, BL, split_axis=1, concat_axis=2, tiled=True)
    col_real, col_imag = dft_last(spread_rows[0], spread_rows[1], -1.0)
    turned = to_columns(jnp.stack([col_real, col_imag]))
    grid_real, grid_imag = dft_last(turned[0], turned[1], -1.0)
    grid_block = jnp.stack([grid_real, grid_imag]) / N
    depth = grid_block.shape[1]
    owned_cols = depth // SUB
    tile_rows = N // SUB
    table = grid_block.reshape(2, owned_cols, SUB, tile_rows, SUB).transpose(1, 3, 0, 4, 2)
    table = table.reshape(owned_cols * tile_rows, 2 * SUB * SUB)
    table_rows = table.shape[0]
    sub_count = tile_slot.shape[0]
    capacity = max(2, 4 * sub_count // groups)
    buckets = groups * capacity
    owner = tile_group[:, 0]
    onehot = (owner[:, None] == jnp.arange(groups, dtype=jnp.int32)[None, :]).astype(jnp.int32)
    rank = jnp.sum(jnp.cumsum(onehot, axis=0) * onehot, axis=1) - 1
    bucket = owner * capacity + rank
    requests = jnp.zeros((buckets,), jnp.int32).at[bucket].set(tile_slot)
    asked = exchange_by_axis(requests, BL, (0, 1), 0, 0)
    fetched = several_exchanges(table[asked], BL, 2, 0, 0)
    mine = fetched[bucket].reshape(sub_count, 2, SUB, SUB)
    residual_vis, contrib = run_blocks(mine, vis_coords, vis_observed, w_plane, vis_count)
    outgoing = jnp.zeros((buckets, 2 * SUB * SUB), jnp.float32).at[bucket].set(contrib)
    arriving = lax.all_to_all(outgoing, BL, split_axis=0, concat_axis=0, tiled=True)
    summed = jax.ops.segment_sum(arriving, asked, num_segments=table_rows)
    resid_block = (
        summed.reshape(owned_cols, tile_rows, 2, SUB, SUB)
        .transpose(2, 0, 4, 1, 3)
        .reshape(2, depth, N)
    )
    inv_real, inv_imag = dft_last(resid_block[0], resid_block[1], 1.0)
    turned_back = to_columns(jnp.stack([inv_real, inv_imag]))
    out_real, out_imag = dft_last(turned_back[0], turned_back[1], 1.0)
    residual_image = several_exchanges(jnp.stack([out_real, out_imag]) / N, BL, 2, 2, 1)
    return (residual_image, residual_vis)


def solution(mesh):
    torus = Mesh(mesh.devices.reshape(mesh.shape["slab"], 8, 4), ("slab", "bl_0", "bl_1"))
    in_specs = (
        P(None, "slab", BL),
        P(SLAB_BL, None, None),
        P(SLAB_BL, None, None),
        P(SLAB_BL),
        P(SLAB_BL, None),
        P(SLAB_BL),
        P(SLAB_BL),
    )
    out_specs = (P(None, "slab", BL), P(SLAB_BL, None, None))
    return jax.shard_map(
        per_device, mesh=torus, in_specs=in_specs, out_specs=out_specs, check_vma=False
    )
```

profile of v0, /device:TPU:1, one launch (start us, length us, event | category | flops | bytes accessed | tf_op | source)
XLA Modules:
  0.0 609.0 jit_solution(571425317024176932)
XLA Ops:
  4.5 9.0 %all-to-all-start = ((s32[8,4,2]{1,2,0:T(2,128)}), s32[8,4,2]{1,2,0:T(2,128)S(1)}, u32[]{:S(2)}, u32[]{:S(2)}) async-start(s32[8,4,2]{1,2,0:T(2,128)} %copy.150), calls=%async_computation | async-start | bytes 16384 | tf_op jit(solution)/shard_map/all_to_all | solution.py:45
  13.5 4.5 copy.153
  20.1 7.5 %all-to-all-start.2 = ((f32[2,1024,256]{2,0,1:T(2,128)}), f32[2,1024,256]{2,0,1:T(2,128)S(1)}, u32[]{:S(2)}, u32[]{:S(2)}) async-start(f32[2,1024,256]{2,0,1:T(2,128)} %copy.153), calls=%async_computation.2 | async-start | bytes 4194304 | tf_op jit(solution)/shard_map/all_to_all | solution.py:201
  28.4 47.1 %all-to-all-done.2 = f32[2,1024,256]{2,0,1:T(2,128)S(1)} async-done(((f32[2,1024,256]{2,0,1:T(2,128)}), f32[2,1024,256]{2,0,1:T(2,128)S(1)}, u32[]{:S(2)}, u32[]{:S(2)}) %all-to-all-start.2) | async-done | bytes 2097184 | tf_op jit(solution)/shard_map/all_to_all | solution.py:201
  75.5 6.1 %all-to-all-start.1 = ((s32[8,4,2]{0,2,1:T(2,128)}), s32[8,4,2]{0,2,1:T(2,128)S(1)}, u32[]{:S(2)}, u32[]{:S(2)}) async-start(s32[8,4,2]{0,2,1:T(2,128)} %copy.151), calls=%async_computation.1 | async-start | bytes 8192 | tf_op jit(solution)/shard_map/all_to_all | solution.py:45
  97.7 4.4 stack.48
  105.1 3.4 fusion.8
  112.7 3.6 copy.158
  117.7 4.3 reshape.354
  122.0 5.1 copy.216
  130.1 11.4 %all-to-all-start.3 = ((f32[256,2,1,1,1024]{4,1,3,2,0:T(2,128)}), f32[256,2,1,1,1024]{4,1,3,2,0:T(2,128)S(1)}, u32[]{:S(2)}, u32[]{:S(2)}) async-start(f32[256,2,1,1,1024]{4,1,3,2,0:T(2,128)} %copy.160), calls=%async_computation.3 | async-start | bytes 4194304 | tf_op jit(solution)/shard_map/all_to_all | solution.py:36
  141.7 53.3 %all-to-all-done.3 = f32[256,2,1,1,1024]{4,1,3,2,0:T(2,128)S(1)} async-done(((f32[256,2,1,1,1024]{4,1,3,2,0:T(2,128)}), f32[256,2,1,1,1024]{4,1,3,2,0:T(2,128)S(1)}, u32[]{:S(2)}, u32[]{:S(2)}) %all-to-all-start.3) | async-done | bytes 2097184 | tf_op jit(solution)/shard_map/all_to_all | solution.py:36
  196.9 4.8 reshape_reshape.19
  201.7 8.5 %fusion.495 = (f32[1,32,8,32,32]{1,4,2,3,0:T(8,128)}, f32[1,32,8,32,32]{1,4,2,3,0:T(8,128)}) fusion(f32[2,32,8,32,32]{1,4,2,3,0:T(8,128)} %bitcast.307), kind=kLoop, calls=%fused_computation.518 | loop fusion | bytes 4194304 | tf_op jit(solution)/shard_map/slice | solution.py:204
  210.2 6.4 %copy.163 = f32[1,32,8,32,32]{4,3,2,1,0:T(8,128)} copy(f32[1,32,8,32,32]{1,4,2,3,0:T(8,128)} %get-tuple-element.23) | data formatting | bytes 2097152 | tf_op jit(solution)/shard_map/slice | solution.py:204
  216.6 3.3 reshape_squeeze.26
  223.2 6.4 %copy.164 = f32[1,32,8,32,32]{4,3,2,1,0:T(8,128)} copy(f32[1,32,8,32,32]{1,4,2,3,0:T(8,128)} %get-tuple-element.22) | data formatting | bytes 2097152 | tf_op jit(solution)/shard_map/slice | solution.py:204
  229.6 3.5 reshape_squeeze.27
  240.2 3.2 copy.165
  243.3 4.3 stack.51
  254.0 8.3 %fusion = f32[1,256,2,32,32]{3,1,4,0,2:T(8,128)} fusion(f32[1,1,32,256,32]{4,3,2,1,0:T(8,128)} %stack.52, f32[1,1,32,256,32]{4,3,2,1,0:T(8,128)} %stack.51), kind=kLoop, calls=%fused_computation.6 | loop fusion | flops 1048576 | bytes 4194304 | tf_op jit(solution)/shard_map/transpose | solution.py:209
  262.4 6.4 %copy.167 = f32[1,256,2,32,32]{1,4,3,2,0:T(8,128)} copy(f32[1,256,2,32,32]{3,1,4,0,2:T(8,128)} %fusion) | data formatting | bytes 4194304 | tf_op jit(solution)/shard_map/transpose | solution.py:209
  273.0 3.9 all-to-all-start.4
  276.9 11.1 %all-to-all-done.4 = f32[32,1,2048]{2,1,0:T(1,128)S(1)} async-done(((f32[32,1,2048]{2,1,0:T(1,128)}), f32[32,1,2048]{2,1,0:T(1,128)S(1)}, u32[]{:S(2)}, u32[]{:S(2)}) %all-to-all-start.4) | async-done | bytes 262176 | tf_op jit(solution)/shard_map/all_to_all | solution.py:65
  288.0 5.1 all-to-all-start.5
  293.2 9.9 %all-to-all-done.5 = f32[32,1,2048]{2,1,0:T(1,128)S(1)} async-done(((f32[32,1,2048]{2,1,0:T(1,128)}), f32[32,1,2048]{2,1,0:T(1,128)S(1)}, u32[]{:S(2)}, u32[]{:S(2)}) %all-to-all-start.5) | async-done | bytes 262176 | tf_op jit(solution)/shard_map/all_to_all | solution.py:65
  316.5 3.3 fusion.78
  340.8 4.1 all-to-all-start.6
  345.2 13.1 %all-to-all-done.6 = f32[32,2,2048]{2,1,0:T(2,128)S(1)} async-done(((f32[32,2,2048]{2,1,0:T(2,128)}), f32[32,2,2048]{2,1,0:T(2,128)S(1)}, u32[]{:S(2)}, u32[]{:S(2)}) %all-to-all-start.6) | async-done | bytes 524320 | tf_op jit(solution)/shard_map/all_to_all | solution.py:225
  367.1 3.3 reshape_squeeze.28
  376.4 3.3 reshape_squeeze.29
  388.7 4.5 stack.57
  396.0 3.4 fusion.4
  403.6 3.6 copy.191
  408.6 4.3 reshape.355
  412.9 5.1 copy.217
  419.7 66.7 %all_to_all.67 = f32[256,2,1,1,1024]{4,1,3,2,0:T(2,128)S(1)} all-to-all(f32[256,2,1,1,1024]{4,1,3,2,0:T(2,128)S(1)} %copy.193), channel_id=1, replica_groups=mesh['slab'=8,'bl_0'=8,'bl_1'=4] {'slab','bl_0','bl_1'}, dimensions={0} | all-to-all | bytes 4194304 | tf_op jit(solution)/shard_map/all_to_all | solution.py:36
  488.2 4.8 reshape_reshape.21
  493.0 8.5 %fusion.494 = (f32[1,32,8,32,32]{1,4,2,3,0:T(8,128)}, f32[1,32,8,32,32]{1,4,2,3,0:T(8,128)}) fusion(f32[2,32,8,32,32]{1,4,2,3,0:T(8,128)} %bitcast.308), kind=kLoop, calls=%fused_computation.517 | loop fusion | bytes 4194304 | tf_op jit(solution)/shard_map/slice | solution.py:234
  501.5 6.4 %copy.196 = f32[1,32,8,32,32]{4,3,2,1,0:T(8,128)} copy(f32[1,32,8,32,32]{1,4,2,3,0:T(8,128)} %get-tuple-element.21) | data formatting | bytes 2097152 | tf_op jit(solution)/shard_map/slice | solution.py:234
  507.9 3.3 reshape_squeeze.30
  514.5 6.4 %copy.197 = f32[1,32,8,32,32]{4,3,2,1,0:T(8,128)} copy(f32[1,32,8,32,32]{1,4,2,3,0:T(8,128)} %get-tuple-element.20) | data formatting | bytes 2097152 | tf_op jit(solution)/shard_map/slice | solution.py:234
  520.9 3.5 reshape_squeeze.31
  535.4 3.4 fusion.2
  545.4 3.9 all-to-all-start.8
  550.9 24.5 %all-to-all-done.8 = f32[32,2,16,256]{3,2,1,0:T(8,128)S(1)} async-done(((f32[32,2,16,256]{3,2,1,0:T(8,128)}), f32[32,2,16,256]{3,2,1,0:T(8,128)S(1)}, u32[]{:S(2)}, u32[]{:S(2)}) %all-to-all-start.8) | async-done | bytes 1048608 | tf_op jit(solution)/shard_map/all_to_all | solution.py:65
  575.4 6.3 %all-to-all-start.9 = ((f32[32,2,16,256]{3,2,1,0:T(8,128)}), f32[32,2,16,256]{3,2,1,0:T(8,128)S(1)}, u32[]{:S(2)}, u32[]{:S(2)}) async-start(f32[32,2,16,256]{3,2,1,0:T(8,128)} %copy.201), calls=%async_computation.9 | async-start | bytes 2097152 | tf_op jit(solution)/shard_map/all_to_all | solution.py:65
  582.4 24.6 %all-to-all-done.9 = f32[32,2,16,256]{3,2,1,0:T(8,128)S(1)} async-done(((f32[32,2,16,256]{3,2,1,0:T(8,128)}), f32[32,2,16,256]{3,2,1,0:T(8,128)S(1)}, u32[]{:S(2)}, u32[]{:S(2)}) %all-to-all-start.9) | async-done | bytes 1048608 | tf_op jit(solution)/shard_map/all_to_all | solution.py:65
  (145 shorter events, 152.4 us)
Async XLA Ops:
  4.5 15.6 %all-to-all-start = ((s32[8,4,2]{1,2,0:T(2,128)}), s32[8,4,2]{1,2,0:T(2,128)S(1)}, u32[]{:S(2)}, u32[]{:S(2)}) async-start(s32[8,4,2]{1,2,0:T(2,128)} %copy.150), calls=%async_computation | async-start | bytes 16384 | tf_op jit(solution)/shard_map/all_to_all | solution.py:45
  20.1 55.4 %all-to-all-start.2 = ((f32[2,1024,256]{2,0,1:T(2,128)}), f32[2,1024,256]{2,0,1:T(2,128)S(1)}, u32[]{:S(2)}, u32[]{:S(2)}) async-start(f32[2,1024,256]{2,0,1:T(2,128)} %copy.153), calls=%async_computation.2 | async-start | bytes 4194304 | tf_op jit(solution)/shard_map/all_to_all | solution.py:201
  75.5 54.5 %all-to-all-start.1 = ((s32[8,4,2]{0,2,1:T(2,128)}), s32[8,4,2]{0,2,1:T(2,128)S(1)}, u32[]{:S(2)}, u32[]{:S(2)}) async-start(s32[8,4,2]{0,2,1:T(2,128)} %copy.151), calls=%async_computation.1 | async-start | bytes 8192 | tf_op jit(solution)/shard_map/all_to_all | solution.py:45
  88.7 1.2 copy-start.3
  130.1 64.9 %all-to-all-start.3 = ((f32[256,2,1,1,1024]{4,1,3,2,0:T(2,128)}), f32[256,2,1,1,1024]{4,1,3,2,0:T(2,128)S(1)}, u32[]{:S(2)}, u32[]{:S(2)}) async-start(f32[256,2,1,1,1024]{4,1,3,2,0:T(2,128)} %copy.160), calls=%async_computation.3 | async-start | bytes 4194304 | tf_op jit(solution)/shard_map/all_to_all | solution.py:36
  233.0 1.2 copy-start
  271.5 5.4 copy-start.7
  271.5 21.7 %copy-start.5 = (f32[16,2,128]{2,1,0:T(2,128)S(1)}, f32[16,2,128]{2,1,0:T(2,128)}, u32[]{:S(2)}) copy-start(f32[16,2,128]{2,1,0:T(2,128)} %param.8) | copy-start | bytes 49156
  273.0 15.0 %all-to-all-start.4 = ((f32[32,1,2048]{2,1,0:T(1,128)}), f32[32,1,2048]{2,1,0:T(1,128)S(1)}, u32[]{:S(2)}, u32[]{:S(2)}) async-start(f32[32,1,2048]{2,1,0:T(1,128)} %get-tuple-element.38), calls=%async_computation.4 | async-start | bytes 524288 | tf_op jit(solution)/shard_map/all_to_all | solution.py:65
  288.0 15.1 %all-to-all-start.5 = ((f32[32,1,2048]{2,1,0:T(1,128)}), f32[32,1,2048]{2,1,0:T(1,128)S(1)}, u32[]{:S(2)}, u32[]{:S(2)}) async-start(f32[32,1,2048]{2,1,0:T(1,128)} %get-tuple-element.39), calls=%async_computation.5 | async-start | bytes 524288 | tf_op jit(solution)/shard_map/all_to_all | solution.py:65
  309.5 10.3 %copy-start.4 = (f32[16,2,128]{2,1,0:T(2,128)S(1)}, f32[16,2,128]{2,1,0:T(2,128)}, u32[]{:S(2)}) copy-start(f32[16,2,128]{2,1,0:T(2,128)} %param.9) | copy-start | bytes 49156
  309.5 10.3 %copy-start.6 = (s32[16]{0:T(128)S(1)}, s32[16]{0:T(128)}, u32[]{:S(2)}) copy-start(s32[16]{0:T(128)} %param.13) | copy-start | bytes 196
  340.8 17.4 %all-to-all-start.6 = ((f32[32,2,2048]{2,1,0:T(2,128)}), f32[32,2,2048]{2,1,0:T(2,128)S(1)}, u32[]{:S(2)}, u32[]{:S(2)}) async-start(f32[32,2,2048]{2,1,0:T(2,128)} %all_to_all.51), calls=%async_computation.6 | async-start | bytes 1048576 | tf_op jit(solution)/shard_map/all_to_all | solution.py:225
  379.7 1.2 copy-start.1
  524.4 1.2 copy-start.2
  545.4 30.0 %all-to-all-start.8 = ((f32[32,2,16,256]{3,2,1,0:T(8,128)}), f32[32,2,16,256]{3,2,1,0:T(8,128)S(1)}, u32[]{:S(2)}, u32[]{:S(2)}) async-start(f32[32,2,16,256]{3,2,1,0:T(8,128)} %copy.200), calls=%async_computation.8 | async-start | bytes 2097152 | tf_op jit(solution)/shard_map/all_to_all | solution.py:65
  575.4 31.5 %all-to-all-start.9 = ((f32[32,2,16,256]{3,2,1,0:T(8,128)}), f32[32,2,16,256]{3,2,1,0:T(8,128)S(1)}, u32[]{:S(2)}, u32[]{:S(2)}) async-start(f32[32,2,16,256]{3,2,1,0:T(8,128)} %copy.201), calls=%async_computation.9 | async-start | bytes 2097152 | tf_op jit(solution)/shard_map/all_to_all | solution.py:65
where the time goes:
time: 617 us; the launch traced here: 609 us
  local copies, waits for them, and re-layouts  192 us (31%)
  waiting for transfers between devices  186 us (30%)
  matrix products  87.4 us (14%)
  blocking collectives  66.7 us (11%)
  starting transfers between devices  57.2 us (9%)
  other arithmetic  18.6 us (3%)
    dot_general x56, matrix products, complex_einsum(): jnp.einsum(form, first, second, precision=lax.Precision.HIGHEST)  87.4 us
    all_to_all x4, waiting for transfers between devices, several_exchanges(): lax.all_to_all(section, axis, split_axis=0, concat_axis=0, tiled=True)  70 us
    all_to_all x1, blocking collectives, joined_exchange(): parts = lax.all_to_all(parts, axis, split_axis=0, concat_axis=0, tiled=True)  66.7 us
    all_to_all x1, waiting for transfers between devices, joined_exchange(): parts = lax.all_to_all(parts, axis, split_axis=0, concat_axis=0, tiled=True)  53.3 us
    all_to_all x1, waiting for transfers between devices, per_device(): lax.all_to_all(model_image, BL, split_axis=1, concat_axis=2, tiled=True)  47.1 us
    slice x3, local copies, waits for them, and re-layouts, per_device(): grid_real, grid_imag = dft_last(turned[0], turned[1], -1.0)  21.3 us
    slice x3, local copies, waits for them, and re-layouts, per_device(): out_real, out_imag = dft_last(turned_back[0], turned_back[1], 1.0)  21.3 us
    all_to_all x4, starting transfers between devices, several_exchanges(): lax.all_to_all(section, axis, split_axis=0, concat_axis=0, tiled=True)  19.2 us
  transfers between devices with their start and end apart: 9, of which 8 were waited for; matrix products, arithmetic and copies ran while one was open for 9% of the time, Pallas kernels for 0%

commit v1 on v0

v1 whole, which is shorter than its diff:
```python
import functools
import math

import jax
import jax.numpy as jnp
import numpy as np
from jax import lax
from jax.experimental import pallas as pl
from jax.experimental.pallas import tpu as pltpu
from jax.sharding import Mesh
from jax.sharding import PartitionSpec as P

N = 8192
SUB = 32
BL = ("bl_0", "bl_1")
SLAB_BL = ("slab", "bl_0", "bl_1")
PLANE = ("slab", "bl_1")
W_STEP = 0.1
F32 = jnp.float32
BF16 = jnp.bfloat16
HIGHEST = lax.Precision.HIGHEST
MESH = pl.DeviceIdType.MESH
ANY = pl.BlockSpec(memory_space=pl.ANY)
DMA = pltpu.SemaphoreType.DMA
VMEM_LIMIT = 62 * 1024 * 1024


def unit(numerator, modulus):
    angle = 2.0 * np.pi * (numerator % modulus) / modulus
    return np.cos(angle), np.sin(angle)


def halves(value):
    high = value.astype(BF16)
    return high, (value - high.astype(F32)).astype(BF16)


def np_halves(value):
    value = np.asarray(value, np.float32)
    high = value.astype(BF16)
    return np.stack([high, (value - high.astype(np.float32)).astype(BF16)])


def row_tables():
    index = np.arange(256)
    cos, sin = unit(np.outer(index, index), 256)
    return np.concatenate([np_halves(cos), np_halves(sin)])


def column_tables():
    a = np.arange(128)[:, None]
    v = np.arange(1024)[None, :]
    cos, sin = unit(a * v, 1024)
    return np.concatenate([np_halves(cos), np_halves(sin)])


def screen_tables():
    b = np.arange(8)[:, None]
    v = np.arange(N)[None, :]
    cos, sin = unit(b * v, N)
    both = np.stack([cos, -sin]).reshape(2, 8, 64, 128)
    return both.transpose(2, 0, 1, 3).astype(np.float32)


def dot(left, right):
    return jnp.dot(left, right, preferred_element_type=F32)


def dot_t(left, right):
    return lax.dot_general(left, right, (((1,), (1,)), ((), ())), preferred_element_type=F32)


def dot3(left, right, product=dot):
    return product(left[0], right[0]) + (product(left[0], right[1]) + product(left[1], right[0]))


def dft4(values, sign):
    (ar, ai), (br, bi), (cr, ci), (dr, di) = values
    pr, pi, mr, mi = ar + cr, ai + ci, ar - cr, ai - ci
    qr, qi, nr, ni = br + dr, bi + di, br - dr, bi - di
    return [
        (pr + qr, pi + qi),
        (mr - sign * ni, mi + sign * nr),
        (pr - qr, pi - qi),
        (mr + sign * ni, mi - sign * nr),
    ]


def turn(value, numerator, modulus, sign):
    cos, sin = math.cos(2 * math.pi * numerator / modulus), sign * math.sin(2 * math.pi * numerator / modulus)
    if numerator % modulus == 0:
        return value
    re, im = value
    return (re * cos - im * sin, re * sin + im * cos)


def dft8(values, sign):
    even, odd = dft4(values[0::2], sign), dft4(values[1::2], sign)
    out = [None] * 8
    for k in range(4):
        tr, ti = turn(odd[k], k, 8, sign)
        out[k] = (even[k][0] + tr, even[k][1] + ti)
        out[k + 4] = (even[k][0] - tr, even[k][1] - ti)
    return out


def butterfly(v_ref, w_ref, rows):
    def tile(step, carry):
        lanes = pl.ds(pl.multiple_of(step * 128, 128), 128)
        mid = []
        for b in range(4):
            column = dft8([(v_ref[s, 0, b, rows, lanes], v_ref[s, 1, b, rows, lanes]) for s in range(8)], -1.0)
            mid.append([turn(column[i0], i0 * b, 32, -1.0) for i0 in range(8)])
        for i0 in range(8):
            done = dft4([mid[b][i0] for b in range(4)], -1.0)
            for i1 in range(4):
                w_ref[i0 + 8 * i1, 0, rows, lanes] = done[i1][0]
                w_ref[i0 + 8 * i1, 1, rows, lanes] = done[i1][1]
        return carry

    lax.fori_loop(0, 2, tile, 0)


def unbutterfly(w_ref, v_ref, rows):
    def tile(step, carry):
        lanes = pl.ds(pl.multiple_of(step * 128, 128), 128)
        mid = []
        for i0 in range(8):
            column = dft4([(w_ref[i0 + 8 * i1, 0, rows, lanes], w_ref[i0 + 8 * i1, 1, rows, lanes]) for i1 in range(4)], 1.0)
            mid.append([turn(column[b], i0 * b, 32, 1.0) for b in range(4)])
        for b in range(4):
            done = dft8([mid[i0][b] for i0 in range(8)], 1.0)
            for s in range(8):
                v_ref[s, 0, b, rows, lanes] = done[s][0]
                v_ref[s, 1, b, rows, lanes] = done[s][1]
        return carry

    lax.fori_loop(0, 2, tile, 0)


def remote(src, dst, send, recv, device):
    return pltpu.make_async_remote_copy(
        src_ref=src, dst_ref=dst, send_sem=send, recv_sem=recv, device_id=device, device_id_type=MESH
    )


def each(count, body):
    def step(at, carry):
        body(at)
        return carry

    lax.fori_loop(1, count, step, 0)


def place_of(peer, z):
    return (peer // 4, z, peer % 4)


def greet(plane, along_z):
    slab, z, x = (lax.axis_index(a) for a in SLAB_BL)
    own = slab * 4 + x
    barrier = pltpu.get_barrier_semaphore()
    if plane:
        each(32, lambda d: pl.semaphore_signal(barrier, inc=1, device_id=place_of((own + d) % 32, z), device_id_type=MESH))
    if along_z:
        each(8, lambda d: pl.semaphore_signal(barrier, inc=1, device_id=(slab, (z + d) % 8, x), device_id_type=MESH))
    pl.semaphore_wait(barrier, 31 * plane + 7 * along_z)
    return slab, z, x, own


def eight(c):
    return pl.ds(8 * c, 8)


def forward_kernel(image_ref, word_ref, a_ref, idx_ref, v_ref, w_ref, zrow_ref, row_ref, local, send1, recv1, send2, recv2, sendz, recvz, sendi, recvi):
    slab, z, x, own = greet(True, True)

    def word_copy(d):
        peer = (z + d) % 8
        return remote(word_ref, zrow_ref.at[z], sendz.at[d], recvz.at[z], (slab, peer, x))

    def slab_copy(c, d):
        peer = (slab + d) % 8
        return remote(image_ref.at[:, :, peer, eight(c)], v_ref.at[slab, :, :, eight(c)], send1.at[c, d], recv1.at[c, slab], (peer, z, x))

    def slab_wait(c, d):
        peer = (slab + d) % 8
        remote(image_ref.at[:, :, peer, eight(c)], v_ref.at[peer, :, :, eight(c)], send1.at[c, d], recv1.at[c, peer], (peer, z, x)).wait_recv()

    def plane_copy(c, d):
        peer = (own + d) % 32
        return remote(w_ref.at[peer, :, eight(c)], a_ref.at[own, :, eight(c)], send2.at[c, d], recv2.at[c, own], place_of(peer, z))

    def plane_wait(c, d):
        peer = (own + d) % 32
        remote(w_ref.at[peer, :, eight(c)], a_ref.at[peer, :, eight(c)], send2.at[c, d], recv2.at[c, peer], place_of(peer, z)).wait_recv()

    def row_copy(d):
        return remote(row_ref, idx_ref.at[own], sendi.at[d], recvi.at[own], place_of((own + d) % 32, z))

    each(8, lambda d: word_copy(d).start())
    mine = pltpu.make_async_copy(image_ref.at[:, :, slab], v_ref.at[slab], local)
    mine.start()
    for c in range(4):
        each(8, lambda d: slab_copy(c, d).start())

    def word_wait(d):
        peer = (z + d) % 8
        remote(word_ref, zrow_ref.at[peer], sendz.at[d], recvz.at[peer], (slab, peer, x)).wait_recv()

    each(8, word_wait)
    zrow_ref[z] = word_ref[...]
    row = zrow_ref[0]
    for at in range(1, 8):
        row = row + zrow_ref[at]
    row_ref[...] = row
    idx_ref[own] = row
    mine.wait()
    for c in range(4):
        each(8, lambda d: slab_wait(c, d))
        if c == 0:
            each(32, lambda d: row_copy(d).start())
        butterfly(v_ref, w_ref, eight(c))
        each(32, lambda d: plane_copy(c, d).start())
        a_ref[own, :, eight(c)] = w_ref[own, :, eight(c)]

    def row_wait(d):
        peer = (own + d) % 32
        remote(row_ref, idx_ref.at[peer], sendi.at[d], recvi.at[peer], place_of(peer, z)).wait_recv()

    each(32, row_wait)
    for c in range(4):
        each(32, lambda d: plane_wait(c, d))
    each(8, lambda d: word_copy(d).wait_send())
    each(32, lambda d: row_copy(d).wait_send())
    for c in range(4):
        each(8, lambda d: slab_copy(c, d).wait_send())
        each(32, lambda d: plane_copy(c, d).wait_send())


def backward_kernel(spot_ref, out_ref, w_ref, v_ref, local, keep, send1, recv1, send2, recv2):
    slab, z, x, own = greet(True, False)

    def plane_copy(c, d):
        peer = (own + d) % 32
        return remote(spot_ref.at[peer, :, eight(c)], w_ref.at[own, :, eight(c)], send1.at[c, d], recv1.at[c, own], place_of(peer, z))

    def plane_wait(c, d):
        peer = (own + d) % 32
        remote(spot_ref.at[peer, :, eight(c)], w_ref.at[peer, :, eight(c)], send1.at[c, d], recv1.at[c, peer], place_of(peer, z)).wait_recv()

    def slab_copy(c, d):
        peer = (slab + d) % 8
        return remote(v_ref.at[peer, :, :, eight(c)], out_ref.at[:, :, slab, eight(c)], send2.at[c, d], recv2.at[c, slab], (peer, z, x))

    def slab_wait(c, d):
        peer = (slab + d) % 8
        remote(v_ref.at[peer, :, :, eight(c)], out_ref.at[:, :, peer, eight(c)], send2.at[c, d], recv2.at[c, peer], (peer, z, x)).wait_recv()

    mine = pltpu.make_async_copy(spot_ref.at[own], w_ref.at[own], local)
    mine.start()
    for c in range(4):
        each(32, lambda d: plane_copy(c, d).start())
    mine.wait()
    kept = []
    for c in range(4):
        each(32, lambda d: plane_wait(c, d))
        unbutterfly(w_ref, v_ref, eight(c))
        each(8, lambda d: slab_copy(c, d).start())
        copy = pltpu.make_async_copy(v_ref.at[slab, :, :, eight(c)], out_ref.at[:, :, slab, eight(c)], keep.at[c])
        copy.start()
        kept.append(copy)
    for c in range(4):
        each(8, lambda d: slab_wait(c, d))
        kept[c].wait()
    for c in range(4):
        each(32, lambda d: plane_copy(c, d).wait_send())
        each(8, lambda d: slab_copy(c, d).wait_send())


def placing(x):
    c0 = lax.broadcasted_iota(jnp.int32, (256, 1024), 0)
    n = lax.broadcasted_iota(jnp.int32, (256, 1024), 1)
    hit = (c0 == 8 * (n & 31) + (n >> 7)) & (((n >> 5) & 3) == x)
    return jnp.where(hit, 1.0, 0.0).astype(BF16)


def spread_screens(w4_ref, w_ref):
    group = lax.broadcasted_iota(jnp.int32, (8, 128), 1) >> 5

    def expand(q, carry):
        for m in range(4):
            mask = group == m
            w_ref[4 * q + m, 0] = jnp.where(mask, w4_ref[q, 0], 0.0)
            w_ref[4 * q + m, 1] = jnp.where(mask, w4_ref[q, 1], 0.0)
        return carry

    lax.fori_loop(0, 64, expand, 0)


def fill_columns(m1_ref, full_ref):
    for h in range(2):
        cos, sin = m1_ref[h], m1_ref[2 + h]
        full_ref[h, 0:128, 0:1024] = cos
        full_ref[h, 0:128, 1024:2048] = -sin
        full_ref[h, 128:256, 0:1024] = sin
        full_ref[h, 128:256, 1024:2048] = cos


def gather_kernel(idx_ref, a_ref, tw_ref, m_ref, m1_ref, w4_ref, phz_ref, out_ref, w_ref, full_ref, high_ref, low_ref, z_ref):
    spread_screens(w4_ref, w_ref)
    fill_columns(m1_ref, full_ref)
    cos, sin = (m_ref[0], m_ref[1]), (m_ref[2], m_ref[3])
    twr = jnp.concatenate([tw_ref[0]] * 2, axis=1)
    twi = jnp.concatenate([tw_ref[1]] * 2, axis=1)
    total = [None] * 4
    for x in range(4):
        ar = a_ref[:, x, 0].reshape(256, 256)
        ai = a_ref[:, x, 1].reshape(256, 256)
        br, bi = halves(ar * twr - ai * twi), halves(ar * twi + ai * twr)
        ur = dot3(cos, br) + dot3(sin, bi)
        ui = dot3(cos, bi) - dot3(sin, br)
        place = placing(x)
        for at, piece in enumerate(halves(ur) + halves(ui)):
            part = dot(piece, place)
            total[at] = part if total[at] is None else total[at] + part
    for b in range(8):
        cut = slice(128 * b, 128 * b + 128)
        rows = pl.ds(b, 256, stride=8)
        for part in range(2):
            high_ref[part, rows, :] = total[2 * part][:, cut]
            low_ref[part, rows, :] = total[2 * part + 1][:, cut]

    def stage(step, carry):
        block, part = step // 4, step % 4
        rows = pl.ds(pl.multiple_of(part * 512, 512), 512)
        lanes = pl.ds(pl.multiple_of(block * 256, 256), 256)
        left = tuple(jnp.concatenate([ref[0, rows, :], ref[1, rows, :]], axis=1).astype(BF16) for ref in (high_ref, low_ref))
        right = (full_ref[0, :, lanes], full_ref[1, :, lanes])
        res = dot3(left, right)
        tus = pl.ds(pl.multiple_of(part * 64, 64), 64)
        z_ref[2 * block, tus] = res[:, 0:128].reshape(64, 8, 128)
        z_ref[2 * block + 1, tus] = res[:, 128:256].reshape(64, 8, 128)
        return carry

    lax.fori_loop(0, 32, stage, 0)

    lane = lax.broadcasted_iota(jnp.int32, (8, 128), 1)
    phr, phi = phz_ref[0:1, :], phz_ref[1:2, :]

    def fold(parts):
        total = jnp.sum(jnp.stack(parts), axis=1)
        total = total + pltpu.roll(total, 64, 1)
        return total + pltpu.roll(total, 32, 1)

    def collect(it, carry):
        both = []
        for half in range(2):
            res, ims = [], []
            for k in range(8):
                word = idx_ref[it % 32, 0, it // 32 * 16 + half * 8 + k]
                tu, tv = word & 255, word >> 8
                t = (tv >> 2) & 7
                zr, zi = z_ref[t, tu], z_ref[8 + t, tu]
                wr, wi = w_ref[tv, 0], w_ref[tv, 1]
                res.append(zr * wr - zi * wi)
                ims.append(zr * wi + zi * wr)
            sr, si = fold(res), fold(ims)
            both += [sr * phr - si * phi, sr * phi + si * phr]
        out = jnp.where(lane < 64, jnp.where(lane < 32, both[0], both[1]), jnp.where(lane < 96, both[2], both[3]))
        out_ref[pl.ds(pl.multiple_of(it * 8, 8), 8), :] = out
        return carry

    lax.fori_loop(0, 256, collect, 0)


def scatter_kernel(idx_ref, c_ref, tw_ref, m_ref, m1_ref, w4_ref, f_ref, out_ref, w_ref, full_ref, l_ref, crep_ref, z0_ref, z1_ref):
    spread_screens(w4_ref, w_ref)
    fill_columns(m1_ref, full_ref)
    spread = dot3(halves(c_ref[...]), (f_ref[0], f_ref[1]))
    for at in range(4):
        crep_ref[at] = spread[:, 128 * at : 128 * at + 128]

    def clear(step, carry):
        tus = pl.ds(pl.multiple_of(step * 16, 16), 16)
        zero = jnp.zeros((16, 16, 8, 128), F32)
        z0_ref[:, tus] = zero
        z1_ref[:, tus] = zero
        return carry

    lax.fori_loop(0, 16, clear, 0)

    def add(it, carry):
        for k in range(16):
            z_ref = (z0_ref, z1_ref)[k % 2]
            half, row = k // 8, k % 8
            word = idx_ref[it % 32, 0, it // 32 * 16 + k]
            tu, tv = word & 255, word >> 8
            t = (tv >> 2) & 7
            cr = jnp.broadcast_to(crep_ref[2 * half, pl.ds(it * 8 + row, 1), :], (8, 128))
            ci = jnp.broadcast_to(crep_ref[2 * half + 1, pl.ds(it * 8 + row, 1), :], (8, 128))
            wr, wi = w_ref[tv, 0], w_ref[tv, 1]
            z_ref[t, tu] += cr * wr + ci * wi
            z_ref[8 + t, tu] += ci * wr - cr * wi
        return carry

    lax.fori_loop(0, 256, add, 0)

    def stage(step, carry):
        tus = pl.ds(pl.multiple_of(step * 32, 32), 32)
        res = None
        for block in range(8):
            lanes = slice(256 * block, 256 * block + 256)
            parts = [(z0_ref[t, tus] + z1_ref[t, tus]).reshape(256, 128) for t in (2 * block, 2 * block + 1)]
            left = halves(jnp.concatenate(parts, axis=1))
            part = dot3(left, (full_ref[0, :, lanes], full_ref[1, :, lanes]), dot_t)
            res = part if res is None else res + part
        rows = pl.ds(pl.multiple_of(step * 256, 256), 256)
        l_ref[0, rows, :], l_ref[1, rows, :] = res[:, 0:128], res[:, 128:256]
        return carry

    lax.fori_loop(0, 8, stage, 0)

    wide = []
    for at in range(2):
        wide += halves(jnp.concatenate([l_ref[at, pl.ds(b, 256, stride=8), :] for b in range(8)], axis=1))
    cos, sin = (m_ref[0], m_ref[1]), (m_ref[2], m_ref[3])
    twr = jnp.concatenate([tw_ref[0]] * 2, axis=1)
    twi = jnp.concatenate([tw_ref[1]] * 2, axis=1)
    for x in range(4):
        place = placing(x)
        pieces = [dot_t(piece, place).astype(BF16) for piece in wide]
        ur, ui = (pieces[0], pieces[1]), (pieces[2], pieces[3])
        ar = dot3(cos, ur) - dot3(sin, ui)
        ai = dot3(cos, ui) + dot3(sin, ur)
        out_ref[:, x, 0] = (ar * twr + ai * twi).reshape(8, 32, 256)
        out_ref[:, x, 1] = (ai * twr - ar * twi).reshape(8, 32, 256)


def hdot(left, right):
    return jnp.dot(left, right, preferred_element_type=F32, precision=HIGHEST)


def hdot_t(left, right):
    return lax.dot_general(left, right, (((1,), (1,)), ((), ())), preferred_element_type=F32, precision=HIGHEST)


def subgrid_kernel(t_ref, right_ref, left_ref, wa_ref, wb_ref, pa_ref, pb_ref, obs_ref, live_ref, vis_ref, g_ref, out_ref, send1, recv1, sendr, recvr, sendl, recvl):
    slab, z, x, own = greet(True, True)
    tiles = jnp.concatenate([t_ref[pl.ds(k, 32, stride=8), :] for k in range(8)], axis=0)
    both = hdot(tiles, right_ref[...])
    rows = []
    for k in range(8):
        cut = slice(32 * k, 32 * k + 32)
        y, iy = both[cut, 0:128], both[cut, 128:256]
        column = jnp.concatenate([jnp.concatenate([y, iy], axis=1), jnp.concatenate([iy, -y], axis=1)], axis=0)
        s_both = hdot(left_ref[0], column)
        s, i_s = s_both[:, 0:128], s_both[:, 128:256]
        wa, wb = wa_ref[k], wb_ref[k]
        weighted = wa * s + wb * i_s
        found, i_found = [], []
        for half in range(2):
            at = k + 8 * half
            ar, ai = pa_ref[0, at], pa_ref[1, at]
            br, bi = pb_ref[0, at], pb_ref[1, at]
            phase = jnp.concatenate([jnp.concatenate([br, bi], axis=1), jnp.concatenate([-bi, br], axis=1)], axis=0)
            part = hdot(weighted[:, 64 * half : 64 * half + 64], phase)
            pr, pi = part[:, 0:128], part[:, 128:256]
            live = live_ref[pl.ds(at, 1), :]
            rr = (obs_ref[pl.ds(2 * at, 1), :] - jnp.sum(ar * pr - ai * pi, axis=0, keepdims=True)) * live
            ri = (obs_ref[pl.ds(2 * at + 1, 1), :] - jnp.sum(ar * pi + ai * pr, axis=0, keepdims=True)) * live
            vis_ref[pl.ds(2 * at, 1), :] = rr
            vis_ref[pl.ds(2 * at + 1, 1), :] = ri
            sr, si = ar * rr + ai * ri, ar * ri - ai * rr
            sent = jnp.concatenate([jnp.concatenate([sr, si], axis=1), jnp.concatenate([-si, sr], axis=1)], axis=0)
            back = hdot_t(sent, phase)
            found.append(back[0:32])
            i_found.append(back[32:64])
        c, ic = jnp.concatenate(found, axis=1), jnp.concatenate(i_found, axis=1)
        r, ir = wa * c - wb * ic, wa * ic + wb * c
        rows.append(hdot(left_ref[1], jnp.concatenate([r, ir], axis=0)))
    tile = hdot_t(jnp.concatenate(rows, axis=0), right_ref[:, 0:128])
    for k in range(8):
        out_ref[pl.ds(k, 32, stride=8), :] = tile[32 * k : 32 * k + 32]

    def block(d):
        return pl.ds(pl.multiple_of(8 * d, 8), 8)

    def plane_copy(d):
        peer = (own + d) % 32
        return remote(out_ref.at[block(peer)], g_ref.at[z, block(own)], send1.at[d], recv1.at[own], place_of(peer, z))

    def plane_wait(d):
        peer = (own + d) % 32
        remote(out_ref.at[block(peer)], g_ref.at[z, block(peer)], send1.at[d], recv1.at[peer], place_of(peer, z)).wait_recv()

    each(32, lambda d: plane_copy(d).start())
    g_ref[z, block(own), :] = out_ref[block(own), :]
    each(32, plane_wait)

    def right_copy(h, u):
        ref = g_ref.at[(z + 8 - h) % 8, pl.ds(64 * u, 64)]
        return remote(ref, ref, sendr.at[h, u], recvr.at[h, u], (slab, (z + 1) % 8, x))

    def left_copy(h, u):
        ref = g_ref.at[(z + h) % 8, pl.ds(64 * u, 64)]
        return remote(ref, ref, sendl.at[h, u], recvl.at[h, u], (slab, (z + 7) % 8, x))

    def right_wait(h, u):
        ref = g_ref.at[(z + 7 - h) % 8, pl.ds(64 * u, 64)]
        remote(ref, ref, sendr.at[h, u], recvr.at[h, u], (slab, (z + 1) % 8, x)).wait_recv()

    def left_wait(h, u):
        ref = g_ref.at[(z + 1 + h) % 8, pl.ds(64 * u, 64)]
        remote(ref, ref, sendl.at[h, u], recvl.at[h, u], (slab, (z + 7) % 8, x)).wait_recv()

    for h in range(4):
        for u in range(4):
            if h:
                right_wait(h - 1, u)
            right_copy(h, u).start()
            if h < 3:
                if h:
                    left_wait(h - 1, u)
                left_copy(h, u).start()
    for u in range(4):
        left_wait(2, u)
        right_wait(3, u)
    each(32, lambda d: plane_copy(d).wait_send())
    for u in range(4):
        for h in range(4):
            right_copy(h, u).wait_send()
            if h < 3:
                left_copy(h, u).wait_send()


def subgrid_tables():
    index = np.arange(SUB)
    cos, sin = unit(index[:, None] * (index[None, :] - SUB // 2), SUB)
    one = np.block([[cos, sin], [-sin, cos]])
    turned = np.block([[-sin, cos], [-cos, -sin]])
    zero = np.zeros_like(one)
    right = np.concatenate([np.block([[one, zero], [zero, one]]), np.block([[turned, zero], [zero, turned]])], axis=1)
    left = np.stack([np.concatenate([cos.T, sin.T], axis=1), np.concatenate([cos, -sin], axis=1)])
    return right.astype(np.float32), (left / (SUB * SUB)).astype(np.float32)


def phases(coords):
    offsets = (jnp.arange(SUB, dtype=jnp.int32) - SUB // 2).astype(F32)
    along = (-2.0 * math.pi / SUB) * coords[:, None, :] * offsets[None, :, None]
    return jnp.stack([jnp.cos(along), jnp.sin(along)])


def in_vmem(count):
    return [pl.BlockSpec(memory_space=pltpu.VMEM)] * count


def call(kernel, out, specs, scratch=(), collective_id=None, out_specs=None):
    return pl.pallas_call(
        kernel,
        out_shape=out,
        in_specs=specs,
        out_specs=out_specs or jax.tree.map(lambda _: pl.BlockSpec(memory_space=pltpu.VMEM), out),
        scratch_shapes=list(scratch),
        compiler_params=pltpu.CompilerParams(
            vmem_limit_bytes=VMEM_LIMIT, collective_id=collective_id, has_side_effects=collective_id is not None
        ),
    )


def f32(*shape):
    return jax.ShapeDtypeStruct(shape, F32)


SMEM = pl.BlockSpec(memory_space=pltpu.SMEM)


def per_device(model_image, vis_coords, vis_observed, tile_slot, tile_group, w_plane, vis_count):
    slab, z, x = (lax.axis_index(a) for a in SLAB_BL)
    word = tile_slot + 256 * (32 * slab + tile_group[:, 0])
    lane = jnp.arange(128, dtype=jnp.int32)
    word_row = jnp.where(lane // 16 == z, jnp.tile(word, 8), 0).reshape(1, 128)
    own = slab * 4 + x
    angle = (2.0 * math.pi / N) * (own * jnp.arange(256, dtype=jnp.int32)).astype(F32)
    tw = jnp.broadcast_to(jnp.stack([jnp.cos(angle), -jnp.sin(angle)])[:, :, None], (2, 256, 128))
    j = jnp.arange(128, dtype=jnp.int32)
    shift = (2.0 * math.pi / 8.0) * (j * z % 8).astype(F32)
    phz = jnp.stack([jnp.cos(shift), -jnp.sin(shift)]) / N
    half, part, jj = j // 64, j // 32 % 2, j % 32
    n = jnp.arange(512, dtype=jnp.int32)
    n_half, n_part, n_jj = n // 256, n // 128 % 2, n % 32
    same = (half[:, None] == n_half[None, :]) & (jj[:, None] == n_jj[None, :])
    pick = jnp.where(part[:, None] == n_part[None, :], phz[0][:, None], jnp.where(part[:, None] == 0, -phz[1][:, None], phz[1][:, None]))
    spread = jnp.where(same, pick, 0.0)
    spread = jnp.stack(halves(spread))
    pa, pb = phases(vis_coords[:, 0, :]), phases(vis_coords[:, 1, :])
    mm = (jnp.arange(SUB, dtype=jnp.int32) - SUB // 2).astype(F32)
    radius = (mm[:, None] ** 2 + mm[None, :] ** 2) / (SUB // 2) ** 2
    turned = -W_STEP * w_plane.astype(F32)[:, None, None] * radius[None]
    lanes = lambda value: jnp.concatenate([value[:8], value[:8], value[8:], value[8:]], axis=2)
    wa, wb = lanes(jnp.cos(turned)), lanes(jnp.sin(turned))
    live = (jnp.arange(128, dtype=jnp.int32)[None, :] < vis_count[:, None]).astype(F32)
    rows, columns, screens = row_tables(), column_tables(), screen_tables()
    right, left = subgrid_tables()

    a, words = call(
        forward_kernel,
        (f32(32, 2, 32, 256), jax.ShapeDtypeStruct((32, 1, 128), jnp.int32)),
        [ANY] + in_vmem(1),
        [
            pltpu.VMEM((8, 2, 4, 32, 256), F32),
            pltpu.VMEM((32, 2, 32, 256), F32),
            pltpu.VMEM((8, 1, 128), jnp.int32),
            pltpu.VMEM((1, 128), jnp.int32),
            DMA,
            DMA((4, 8)),
            DMA((4, 8)),
            DMA((4, 32)),
            DMA((4, 32)),
            DMA((8,)),
            DMA((8,)),
            DMA((32,)),
            DMA((32,)),
        ],
        collective_id=0,
    )(model_image.reshape(2, 4, 8, 32, 256), word_row)
    a = a.reshape(8, 4, 2, 32, 256)
    partial = call(
        gather_kernel,
        f32(2048, 128),
        [SMEM] + in_vmem(6),
        [
            pltpu.VMEM((256, 2, 8, 128), F32),
            pltpu.VMEM((2, 256, 2048), BF16),
            pltpu.VMEM((2, 2048, 128), F32),
            pltpu.VMEM((2, 2048, 128), F32),
            pltpu.VMEM((16, 256, 8, 128), F32),
        ],
    )(words, a, tw, rows, columns, screens, phz)
    summed = lax.psum_scatter(partial.reshape(8, 256, 128), "bl_0", scatter_dimension=0, tiled=True)
    tiles = lax.all_to_all(summed.reshape(32, 8, 128), PLANE, split_axis=0, concat_axis=0, tiled=True)
    vis, every = call(
        subgrid_kernel,
        (f32(32, 128), f32(8, 256, 128)),
        in_vmem(9),
        [pltpu.VMEM((256, 128), F32), DMA((32,)), DMA((32,)), DMA((4, 4)), DMA((4, 4)), DMA((3, 4)), DMA((3, 4))],
        collective_id=1,
    )(
        tiles.reshape(256, 128), right, left, wa, wb, pa, pb, vis_observed.reshape(32, 128), live
    )
    every = every.reshape(2048, 128)
    spots = call(
        scatter_kernel,
        f32(8, 4, 2, 32, 256),
        [SMEM] + in_vmem(6),
        [
            pltpu.VMEM((256, 2, 8, 128), F32),
            pltpu.VMEM((2, 256, 2048), BF16),
            pltpu.VMEM((2, 2048, 128), F32),
            pltpu.VMEM((4, 2048, 128), F32),
            pltpu.VMEM((16, 256, 8, 128), F32),
            pltpu.VMEM((16, 256, 8, 128), F32),
        ],
    )(words, every, tw, rows, columns, screens, spread)
    image = call(
        backward_kernel,
        f32(2, 4, 8, 32, 256),
        [ANY],
        [
            pltpu.VMEM((32, 2, 32, 256), F32),
            pltpu.VMEM((8, 2, 4, 32, 256), F32),
            DMA,
            DMA((4,)),
            DMA((4, 32)),
            DMA((4, 32)),
            DMA((4, 8)),
            DMA((4, 8)),
        ],
        collective_id=2,
        out_specs=ANY,
    )(spots.reshape(32, 2, 32, 256)).reshape(2, 1024, 256)
    return image, vis.reshape(16, 2, 128)


def solution(mesh):
    torus = Mesh(mesh.devices.reshape(mesh.shape["slab"], 8, 4), SLAB_BL)
    in_specs = (
        P(None, "slab", BL),
        P(SLAB_BL, None, None),
        P(SLAB_BL, None, None),
        P(SLAB_BL),
        P(SLAB_BL, None),
        P(SLAB_BL),
        P(SLAB_BL),
    )
    out_specs = (P(None, "slab", BL), P(SLAB_BL, None, None))
    return jax.shard_map(per_device, mesh=torus, in_specs=in_specs, out_specs=out_specs, check_vma=False)
```

time: 617 us -> 345 us (0.56); the launches traced: 609 us -> 345 us
  Pallas kernels: 0 us -> 274 us
  local copies, waits for them, and re-layouts: 192 us -> 5.29 us
  waiting for transfers between devices: 186 us -> 29.8 us
  matrix products: 87.4 us -> 0 us
  blocking collectives: 66.7 us -> 0 us
  starting transfers between devices: 57.2 us -> 12.5 us
  between operations: 1.75 us -> 14.2 us
  other arithmetic: 18.6 us -> 9.3 us
    pallas_call x0 -> x5, Pallas kernels: none -> 274 us  [the longest x1 75.3 us: per_device(): call(gather_kernel, f32(2048, 128), [SMEM] + in_vmem(6), [pltpu.VMEM((256...]
    all_to_all x9 -> x1, waiting for transfers between devices: 186 us -> 6.05 us  [per_device(): lax.all_to_all(summed.reshape(32, 8, 128), PLANE, split_axis=0, concat_ax...]
    another operation x31 -> x2, local copies, waits for them, and re-layouts: 87.7 us -> 0.09 us  [per_device(): word_row = jnp.where(lane // 16 == z, jnp.tile(word, 8), 0).reshape(1, 128)]
    dot_general x56 -> x0, matrix products: 87.4 us -> none  [complex_einsum(): jnp.einsum(form, first, second, precision=lax.Precision.HIGHEST)]
    all_to_all x1 -> x0, blocking collectives: 66.7 us -> none  [joined_exchange(): parts = lax.all_to_all(parts, axis, split_axis=0, concat_axis=0, tiled=True)]
    slice x10 -> x2, local copies, waits for them, and re-layouts: 50.7 us -> 0.04 us  [the longest x1 0.04 us: per_device(): value[:8]]
    all_to_all x9 -> x1, starting transfers between devices: 57.2 us -> 12.5 us  [per_device(): lax.all_to_all(summed.reshape(32, 8, 128), PLANE, split_axis=0, concat_ax...]
    reduce_scatter x0 -> x1, waiting for transfers between devices: none -> 23.7 us  [per_device(): lax.psum_scatter(partial.reshape(8, 256, 128), 'bl_0', scatter_dimension=...]
  transfers between devices with their start and end apart: 9 -> 2, of which waited for: 8 -> 2; matrix products, arithmetic and copies ran while one was open for 9% -> 2% of each run, Pallas kernels for 0% -> 0%
where the time goes in v1:
time: 345 us
  Pallas kernels  274 us (79%)
  waiting for transfers between devices  29.8 us (9%)
  between operations  14.2 us (4%)
  starting transfers between devices  12.5 us (4%)
  other arithmetic  9.3 us (3%)
  local copies, waits for them, and re-layouts  5.29 us (2%)
    pallas_call x1, Pallas kernels, per_device(): call(gather_kernel, f32(2048, 128), [SMEM] + in_vmem(6), [pltpu.VMEM((256...  75.3 us
    pallas_call x1, Pallas kernels, per_device(): call(forward_kernel, (f32(32, 2, 32, 256), jax.ShapeDtypeStruct((32, 1, 1...  66.8 us
    pallas_call x1, Pallas kernels, per_device(): call(backward_kernel, f32(2, 4, 8, 32, 256), [ANY], [pltpu.VMEM((32, 2, 3...  56.7 us
    pallas_call x1, Pallas kernels, per_device(): call(scatter_kernel, f32(8, 4, 2, 32, 256), [SMEM] + in_vmem(6), [pltpu.V...  42.1 us
    pallas_call x1, Pallas kernels, per_device(): call(subgrid_kernel, (f32(32, 128), f32(8, 256, 128)), in_vmem(9), [pltpu...  32.5 us
    reduce_scatter x1, waiting for transfers between devices, per_device(): lax.psum_scatter(partial.reshape(8, 256, 128), 'bl_0', scatter_dimension=...  23.7 us
    all_to_all x1, starting transfers between devices, per_device(): lax.all_to_all(summed.reshape(32, 8, 128), PLANE, split_axis=0, concat_ax...  12.5 us
  transfers between devices with their start and end apart: 2, of which 2 were waited for; matrix products, arithmetic and copies ran while one was open for 2% of the time, Pallas kernels for 0%

profile of v1, /device:TPU:1, one launch (start us, length us, event | category | flops | bytes accessed | tf_op | source)
XLA Modules:
  0.0 344.7 jit_solution(10622760966373026879)
XLA Ops:
  7.2 0.0 reduce-scatter.2.cloned.1.call-start
  7.2 0.1 sine_negate_fusion
  7.3 0.1 sine_negate_fusion.1
  7.3 0.7 bitcast_add_fusion
  8.0 0.1 tile.10
  8.1 0.5 compare_select_fusion.5.word_ref
  8.6 0.6 maximum_multiply_fusion.phz_ref
  9.2 66.8 %shard_map.131 = (f32[32,2,32,256]{3,2,1,0:T(8,128)}, s32[32,1,128]{2,1,0:T(1,128)}) custom-call(f32[2,4,8,32,256]{4,3,2,1,0:T(8,128)} %bitcast.21, s32[1,128]{1,0:T(1,128)} %compare_select_fusion.5.word_ref), custom_call_target="tpu_custom_call" | custom-call | tf_op jit(solution)/shard_map/pallas_call | solution.py:606
  76.0 0.8 broadcast_in_dim.17.tw_ref
  76.8 0.0 copy-start.5
  76.8 75.3 %shard_map.132 = f32[2048,128]{1,0:T(8,128)} custom-call(s32[32,1,128]{2,1,0:T(1,128)} %get-tuple-element.6.idx_ref, f32[8,4,2,32,256]{4,3,2,1,0:T(8,128)} %bitcast.22, f32[2,256,128]{2,1,0:T(8,128)} %broadcast_in_dim.17.tw_ref, bf16[4,256,256]{2,1,0:T(8,128)(2,1)} %constant.167.clone.m_ref, bf16[4,128,1024]{2,1,0:T(8,128)(2,1)} %constant.168.clone.m1_ref, ...), custom_call_target="tpu_custom_call" | custom-call | tf_op jit(solution)/shard_map/pallas_call | solution.py:628
  152.2 0.0 copy-start.1
  152.2 0.0 reduce-scatter.2.cloned.1.call-update
  152.3 0.1 add_multiply_fusion
  152.3 0.0 copy-done.5
  152.3 1.0 multiply_sine_fusion.2
  153.3 0.0 copy-start.3
  153.4 0.0 copy-start.4
  153.4 0.8 pad_maximum_fusion.3.wa_ref
  154.2 0.0 copy-done.1
  154.3 1.9 multiply_cosine_fusion
  156.2 1.1 pad_maximum_fusion
  157.2 0.0 copy-done.3
  157.2 0.0 copy-done.4
  157.2 0.7 fusion.1.live_ref
  157.9 0.2 fusion
  158.1 0.2 subtract_convert_fusion
  158.2 23.7 %reduce-scatter.2.cloned.1.call-done = f32[1,256,128]{2,1,0:T(8,128)} async-done(((f32[8,256,128]{2,1,0:T(8,128)}), f32[1,256,128]{2,1,0:T(8,128)}) %reduce-scatter.2.cloned.1.call-update) | async-done | bytes 131088 | tf_op jit(solution)/shard_map/reduce_scatter | solution.py:640
  182.0 12.5 %all-to-all-start = ((f32[32,8,128]{2,1,0:T(8,128)}), f32[32,8,128]{2,1,0:T(8,128)S(1)}, u32[]{:S(2)}, u32[]{:S(2)}) async-start(f32[32,8,128]{2,1,0:T(8,128)} %bitcast.25), calls=%async_computation.1 | async-start | bytes 262144 | tf_op jit(solution)/shard_map/all_to_all | solution.py:641
  194.5 0.8 pad_maximum_fusion.4.wb_ref
  195.3 0.7 pad_maximum_fusion.2.f_ref
  196.0 6.0 %all-to-all-done = f32[32,8,128]{2,1,0:T(8,128)S(1)} async-done(((f32[32,8,128]{2,1,0:T(8,128)}), f32[32,8,128]{2,1,0:T(8,128)S(1)}, u32[]{:S(2)}, u32[]{:S(2)}) %all-to-all-start) | async-done | bytes 131104 | tf_op jit(solution)/shard_map/all_to_all | solution.py:641
  202.1 0.0 copy-start
  202.1 0.7 copy-done
  202.7 32.5 %shard_map.133 = (f32[32,128]{1,0:T(8,128)}, f32[8,256,128]{2,1,0:T(8,128)}) custom-call(f32[256,128]{1,0:T(8,128)} %bitcast.24, f32[128,256]{1,0:T(8,128)} %constant.170.clone.right_ref, f32[2,32,64]{2,1,0:T(8,128)} %constant.171.clone.left_ref, f32[8,32,128]{2,1,0:T(8,128)} %pad_maximum_fusion.3.wa_ref, f32[8,32,128]{2,1,0:T(8,128)} %pad_maximum_fusion.4.wb_ref, ...), custom_call_target="tpu_custom_call" | custom-call | tf_op jit(solution)/shard_map/pallas_call | solution.py:642
  235.3 42.1 %shard_map.134 = f32[8,4,2,32,256]{4,3,2,1,0:T(8,128)} custom-call(s32[32,1,128]{2,1,0:T(1,128)} %get-tuple-element.6.idx_ref, f32[2048,128]{1,0:T(8,128)} %bitcast.23, f32[2,256,128]{2,1,0:T(8,128)} %broadcast_in_dim.17.tw_ref, bf16[4,256,256]{2,1,0:T(8,128)(2,1)} %constant.167.clone.m_ref, bf16[4,128,1024]{2,1,0:T(8,128)(2,1)} %constant.168.clone.m1_ref, ...), custom_call_target="tpu_custom_call" | custom-call | tf_op jit(solution)/shard_map/pallas_call | solution.py:652
  277.4 56.7 %shard_map.135 = f32[2,4,8,32,256]{4,3,2,1,0:T(8,128)} custom-call(f32[32,2,32,256]{3,2,1,0:T(8,128)} %bitcast.19), custom_call_target="tpu_custom_call" | custom-call | tf_op jit(solution)/shard_map/pallas_call | solution.py:665
  334.1 0.0 copy-start.2
  334.2 3.0 copy.16
  337.2 0.0 copy-done.2
  337.2 0.6 copy.17
  (13 shorter events, 0.1 us)
Async XLA Ops:
  7.2 174.8 %reduce-scatter.2.cloned.1.call-start = ((), (), s32[]{:S(2)}) async-start(), calls=%async_computation.2 | async-start | bytes 1179648 | tf_op jit(solution)/shard_map/reduce_scatter | solution.py:640
  76.8 75.5 %copy-start.5 = (s32[16]{0:T(128)S(1)}, s32[16]{0:T(128)}, u32[]{:S(2)}) copy-start(s32[16]{0:T(128)} %param.17) | copy-start | bytes 196
  152.2 2.1 copy-start.1
  153.3 3.9 %copy-start.3 = (f32[2,128]{1,0:T(2,128)S(1)}, f32[2,128]{1,0:T(2,128)}, u32[]{:S(2)}) copy-start(f32[2,128]{1,0:T(2,128)} %maximum_multiply_fusion.phz_ref) | copy-start | bytes 3076
  153.4 3.9 %copy-start.4 = (s32[16]{0:T(128)S(1)}, s32[16]{0:T(128)}, u32[]{:S(2)}) copy-start(s32[16]{0:T(128)} %param.18) | copy-start | bytes 196
  182.0 20.1 %all-to-all-start = ((f32[32,8,128]{2,1,0:T(8,128)}), f32[32,8,128]{2,1,0:T(8,128)S(1)}, u32[]{:S(2)}, u32[]{:S(2)}) async-start(f32[32,8,128]{2,1,0:T(8,128)} %bitcast.25), calls=%async_computation.1 | async-start | bytes 262144 | tf_op jit(solution)/shard_map/all_to_all | solution.py:641
  202.1 0.7 copy-start
  334.1 3.1 copy-start.2
Sparse Core Ops, SparseCore 0:
  152.3 29.6 reduce-scatter.1

commit v2 on v1

--- a/solution.py
+++ b/solution.py
@@ -104,9 +104,10 @@
     return out
 
 
-def butterfly(v_ref, w_ref, rows):
+def butterfly(v_ref, w_ref, c):
     def tile(step, carry):
-        lanes = pl.ds(pl.multiple_of(step * 128, 128), 128)
+        rows = pl.ds(pl.multiple_of(32 // CHUNKS * c + step // 2 * 8, 8), 8)
+        lanes = pl.ds(pl.multiple_of(step % 2 * 128, 128), 128)
         mid = []
         for b in range(4):
             column = dft8([(v_ref[s, 0, b, rows, lanes], v_ref[s, 1, b, rows, lanes]) for s in range(8)], -1.0)
@@ -118,12 +119,13 @@
                 w_ref[i0 + 8 * i1, 1, rows, lanes] = done[i1][1]
         return carry
 
-    lax.fori_loop(0, 2, tile, 0)
-
-
-def unbutterfly(w_ref, v_ref, rows):
+    lax.fori_loop(0, 8 // CHUNKS, tile, 0)
+
+
+def unbutterfly(w_ref, v_ref, c):
     def tile(step, carry):
-        lanes = pl.ds(pl.multiple_of(step * 128, 128), 128)
+        rows = pl.ds(pl.multiple_of(32 // CHUNKS * c + step // 2 * 8, 8), 8)
+        lanes = pl.ds(pl.multiple_of(step % 2 * 128, 128), 128)
         mid = []
         for i0 in range(8):
             column = dft4([(w_ref[i0 + 8 * i1, 0, rows, lanes], w_ref[i0 + 8 * i1, 1, rows, lanes]) for i1 in range(4)], 1.0)
@@ -135,7 +137,7 @@
                 v_ref[s, 1, b, rows, lanes] = done[s][1]
         return carry
 
-    lax.fori_loop(0, 2, tile, 0)
+    lax.fori_loop(0, 8 // CHUNKS, tile, 0)
 
 
 def remote(src, dst, send, recv, device):
@@ -168,8 +170,13 @@
     return slab, z, x, own
 
 
-def eight(c):
-    return pl.ds(8 * c, 8)
+CHUNKS = 2
+STEP8 = 3
+STEP32 = 13
+
+
+def chunk(c):
+    return pl.ds(32 // CHUNKS * c, 32 // CHUNKS)
 
 
 def forward_kernel(image_ref, word_ref, a_ref, idx_ref, v_ref, w_ref, zrow_ref, row_ref, local, send1, recv1, send2, recv2, sendz, recvz, sendi, recvi):
@@ -180,20 +187,20 @@
         return remote(word_ref, zrow_ref.at[z], sendz.at[d], recvz.at[z], (slab, peer, x))
 
     def slab_copy(c, d):
-        peer = (slab + d) % 8
-        return remote(image_ref.at[:, :, peer, eight(c)], v_ref.at[slab, :, :, eight(c)], send1.at[c, d], recv1.at[c, slab], (peer, z, x))
+        peer = (slab + STEP8 * d) % 8
+        return remote(image_ref.at[:, :, peer, chunk(c)], v_ref.at[slab, :, :, chunk(c)], send1.at[c, d], recv1.at[c, slab], (peer, z, x))
 
     def slab_wait(c, d):
-        peer = (slab + d) % 8
-        remote(image_ref.at[:, :, peer, eight(c)], v_ref.at[peer, :, :, eight(c)], send1.at[c, d], recv1.at[c, peer], (peer, z, x)).wait_recv()
+        peer = (slab + STEP8 * d) % 8
+        remote(image_ref.at[:, :, peer, chunk(c)], v_ref.at[peer, :, :, chunk(c)], send1.at[c, d], recv1.at[c, peer], (peer, z, x)).wait_recv()
 
     def plane_copy(c, d):
-        peer = (own + d) % 32
-        return remote(w_ref.at[peer, :, eight(c)], a_ref.at[own, :, eight(c)], send2.at[c, d], recv2.at[c, own], place_of(peer, z))
+        peer = (own + STEP32 * d) % 32
+        return remote(w_ref.at[peer, :, chunk(c)], a_ref.at[own, :, chunk(c)], send2.at[c, d], recv2.at[c, own], place_of(peer, z))
 
     def plane_wait(c, d):
-        peer = (own + d) % 32
-        remote(w_ref.at[peer, :, eight(c)], a_ref.at[peer, :, eight(c)], send2.at[c, d], recv2.at[c, peer], place_of(peer, z)).wait_recv()
+        peer = (own + STEP32 * d) % 32
+        remote(w_ref.at[peer, :, chunk(c)], a_ref.at[peer, :, chunk(c)], send2.at[c, d], recv2.at[c, peer], place_of(peer, z)).wait_recv()
 
     def row_copy(d):
         return remote(row_ref, idx_ref.at[own], sendi.at[d], recvi.at[own], place_of((own + d) % 32, z))
@@ -201,7 +208,7 @@
     each(8, lambda d: word_copy(d).start())
     mine = pltpu.make_async_copy(image_ref.at[:, :, slab], v_ref.at[slab], local)
     mine.start()
-    for c in range(4):
+    for c in range(CHUNKS):
         each(8, lambda d: slab_copy(c, d).start())
 
     def word_wait(d):
@@ -216,24 +223,24 @@
     row_ref[...] = row
     idx_ref[own] = row
     mine.wait()
-    for c in range(4):
+    for c in range(CHUNKS):
         each(8, lambda d: slab_wait(c, d))
         if c == 0:
             each(32, lambda d: row_copy(d).start())
-        butterfly(v_ref, w_ref, eight(c))
+        butterfly(v_ref, w_ref, c)
         each(32, lambda d: plane_copy(c, d).start())
-        a_ref[own, :, eight(c)] = w_ref[own, :, eight(c)]
+        a_ref[own, :, chunk(c)] = w_ref[own, :, chunk(c)]
 
     def row_wait(d):
-        peer = (own + d) % 32
+        peer = (own + STEP32 * d) % 32
         remote(row_ref, idx_ref.at[peer], sendi.at[d], recvi.at[peer], place_of(peer, z)).wait_recv()
 
     each(32, row_wait)
-    for c in range(4):
+    for c in range(CHUNKS):
         each(32, lambda d: plane_wait(c, d))
     each(8, lambda d: word_copy(d).wait_send())
     each(32, lambda d: row_copy(d).wait_send())
-    for c in range(4):
+    for c in range(CHUNKS):
         each(8, lambda d: slab_copy(c, d).wait_send())
         each(32, lambda d: plane_copy(c, d).wait_send())
 
@@ -242,38 +249,38 @@
     slab, z, x, own = greet(True, False)
 
     def plane_copy(c, d):
-        peer = (own + d) % 32
-        return remote(spot_ref.at[peer, :, eight(c)], w_ref.at[own, :, eight(c)], send1.at[c, d], recv1.at[c, own], place_of(peer, z))
+        peer = (own + STEP32 * d) % 32
+        return remote(spot_ref.at[peer, :, chunk(c)], w_ref.at[own, :, chunk(c)], send1.at[c, d], recv1.at[c, own], place_of(peer, z))
 
     def plane_wait(c, d):
-        peer = (own + d) % 32
-        remote(spot_ref.at[peer, :, eight(c)], w_ref.at[peer, :, eight(c)], send1.at[c, d], recv1.at[c, peer], place_of(peer, z)).wait_recv()
+        peer = (own + STEP32 * d) % 32
+        remote(spot_ref.at[peer, :, chunk(c)], w_ref.at[peer, :, chunk(c)], send1.at[c, d], recv1.at[c, peer], place_of(peer, z)).wait_recv()
 
     def slab_copy(c, d):
-        peer = (slab + d) % 8
-        return remote(v_ref.at[peer, :, :, eight(c)], out_ref.at[:, :, slab, eight(c)], send2.at[c, d], recv2.at[c, slab], (peer, z, x))
+        peer = (slab + STEP8 * d) % 8
+        return remote(v_ref.at[peer, :, :, chunk(c)], out_ref.at[:, :, slab, chunk(c)], send2.at[c, d], recv2.at[c, slab], (peer, z, x))
 
     def slab_wait(c, d):
-        peer = (slab + d) % 8
-        remote(v_ref.at[peer, :, :, eight(c)], out_ref.at[:, :, peer, eight(c)], send2.at[c, d], recv2.at[c, peer], (peer, z, x)).wait_recv()
+        peer = (slab + STEP8 * d) % 8
+        remote(v_ref.at[peer, :, :, chunk(c)], out_ref.at[:, :, peer, chunk(c)], send2.at[c, d], recv2.at[c, peer], (peer, z, x)).wait_recv()
 
     mine = pltpu.make_async_copy(spot_ref.at[own], w_ref.at[own], local)
     mine.start()
-    for c in range(4):
+    for c in range(CHUNKS):
         each(32, lambda d: plane_copy(c, d).start())
     mine.wait()
     kept = []
-    for c in range(4):
+    for c in range(CHUNKS):
         each(32, lambda d: plane_wait(c, d))
-        unbutterfly(w_ref, v_ref, eight(c))
+        unbutterfly(w_ref, v_ref, c)
         each(8, lambda d: slab_copy(c, d).start())
-        copy = pltpu.make_async_copy(v_ref.at[slab, :, :, eight(c)], out_ref.at[:, :, slab, eight(c)], keep.at[c])
+        copy = pltpu.make_async_copy(v_ref.at[slab, :, :, chunk(c)], out_ref.at[:, :, slab, chunk(c)], keep.at[c])
         copy.start()
         kept.append(copy)
-    for c in range(4):
+    for c in range(CHUNKS):
         each(8, lambda d: slab_wait(c, d))
         kept[c].wait()
-    for c in range(4):
+    for c in range(CHUNKS):
         each(32, lambda d: plane_copy(c, d).wait_send())
         each(8, lambda d: slab_copy(c, d).wait_send())
 
@@ -307,20 +314,38 @@
         full_ref[h, 128:256, 1024:2048] = cos
 
 
-def gather_kernel(idx_ref, a_ref, tw_ref, m_ref, m1_ref, w4_ref, phz_ref, out_ref, w_ref, full_ref, high_ref, low_ref, z_ref):
+def row_sums(values):
+    at = lax.broadcasted_iota(jnp.int32, (8, 128), 0)
+    quads = []
+    for r in range(4):
+        first, second = values[r], values[r + 4]
+        quads.append(jnp.where(at < 4, first, second) + pltpu.roll(jnp.where(at < 4, second, first), 4, 0))
+    pairs = []
+    for r in range(2):
+        first, second = quads[r] + pltpu.roll(quads[r], 6, 0), quads[r + 2] + pltpu.roll(quads[r + 2], 2, 0)
+        pairs.append(jnp.where(at & 2 == 0, first, second))
+    first, second = pairs[0] + pltpu.roll(pairs[0], 7, 0), pairs[1] + pltpu.roll(pairs[1], 1, 0)
+    return jnp.where(at & 1 == 0, first, second)
+
+
+def gather_kernel(
+    idx_ref, a_ref, tw_ref, m_ref, m1_ref, w4_ref, f_ref, out_ref,
+    w_ref, full_ref, high_ref, low_ref, z_ref, s_ref, part_ref, got_ref, sum_ref, sendz, recvz, sendp, recvp,
+):
+    slab, z, x, own = greet(True, True)
     spread_screens(w4_ref, w_ref)
     fill_columns(m1_ref, full_ref)
     cos, sin = (m_ref[0], m_ref[1]), (m_ref[2], m_ref[3])
     twr = jnp.concatenate([tw_ref[0]] * 2, axis=1)
     twi = jnp.concatenate([tw_ref[1]] * 2, axis=1)
     total = [None] * 4
-    for x in range(4):
-        ar = a_ref[:, x, 0].reshape(256, 256)
-        ai = a_ref[:, x, 1].reshape(256, 256)
+    for xx in range(4):
+        ar = a_ref[:, xx, 0].reshape(256, 256)
+        ai = a_ref[:, xx, 1].reshape(256, 256)
         br, bi = halves(ar * twr - ai * twi), halves(ar * twi + ai * twr)
         ur = dot3(cos, br) + dot3(sin, bi)
         ui = dot3(cos, bi) - dot3(sin, br)
-        place = placing(x)
+        place = placing(xx)
         for at, piece in enumerate(halves(ur) + halves(ui)):
             part = dot(piece, place)
             total[at] = part if total[at] is None else total[at] + part
@@ -338,40 +363,72 @@
         left = tuple(jnp.concatenate([ref[0, rows, :], ref[1, rows, :]], axis=1).astype(BF16) for ref in (high_ref, low_ref))
         right = (full_ref[0, :, lanes], full_ref[1, :, lanes])
         res = dot3(left, right)
-        tus = pl.ds(pl.multiple_of(part * 64, 64), 64)
-        z_ref[2 * block, tus] = res[:, 0:128].reshape(64, 8, 128)
-        z_ref[2 * block + 1, tus] = res[:, 128:256].reshape(64, 8, 128)
+        z_ref[block // 4, pl.ds(pl.multiple_of(block % 4 * 512 + part * 64, 64), 64)] = res[:, 0:128].reshape(64, 8, 128)
+        z_ref[block // 4, pl.ds(pl.multiple_of(block % 4 * 512 + 256 + part * 64, 64), 64)] = res[:, 128:256].reshape(64, 8, 128)
         return carry
 
     lax.fori_loop(0, 32, stage, 0)
 
-    lane = lax.broadcasted_iota(jnp.int32, (8, 128), 1)
-    phr, phi = phz_ref[0:1, :], phz_ref[1:2, :]
-
-    def fold(parts):
-        total = jnp.sum(jnp.stack(parts), axis=1)
-        total = total + pltpu.roll(total, 64, 1)
-        return total + pltpu.roll(total, 32, 1)
-
-    def collect(it, carry):
-        both = []
-        for half in range(2):
-            res, ims = [], []
-            for k in range(8):
-                word = idx_ref[it % 32, 0, it // 32 * 16 + half * 8 + k]
-                tu, tv = word & 255, word >> 8
-                t = (tv >> 2) & 7
-                zr, zi = z_ref[t, tu], z_ref[8 + t, tu]
-                wr, wi = w_ref[tv, 0], w_ref[tv, 1]
-                res.append(zr * wr - zi * wi)
-                ims.append(zr * wi + zi * wr)
-            sr, si = fold(res), fold(ims)
-            both += [sr * phr - si * phi, sr * phi + si * phr]
-        out = jnp.where(lane < 64, jnp.where(lane < 32, both[0], both[1]), jnp.where(lane < 96, both[2], both[3]))
-        out_ref[pl.ds(pl.multiple_of(it * 8, 8), 8), :] = out
-        return carry
-
-    lax.fori_loop(0, 256, collect, 0)
+    def collect(zc):
+        def some(step, carry):
+            for d in (2 * step, 2 * step + 1):
+                for half in range(2):
+                    res, ims = [], []
+                    for k in range(8):
+                        word = idx_ref[d, 0, zc * 16 + half * 8 + k]
+                        spot, tv = word & 2047, word >> 11
+                        zr, zi = z_ref[0, spot], z_ref[1, spot]
+                        wr, wi = w_ref[tv, 0], w_ref[tv, 1]
+                        res.append(zr * wr - zi * wi)
+                        ims.append(zr * wi + zi * wr)
+                    rows = pl.ds(pl.multiple_of(d * 8, 8), 8)
+                    s_ref[2 * half, rows, :] = row_sums(res)
+                    s_ref[2 * half + 1, rows, :] = row_sums(ims)
+            return carry
+
+        lax.fori_loop(0, 16, some, 0)
+        sums = jnp.concatenate([s_ref[at] for at in range(4)], axis=1)
+        part_ref[zc] = dot3(halves(sums), (f_ref[0], f_ref[1]), dot_t)
+
+    def z_copy(d):
+        peer = (z + d) % 8
+        return remote(part_ref.at[peer], got_ref.at[z], sendz.at[d], recvz.at[z], (slab, peer, x))
+
+    def z_wait(d):
+        peer = (z + d) % 8
+        remote(part_ref.at[peer], got_ref.at[peer], sendz.at[d], recvz.at[peer], (slab, peer, x)).wait_recv()
+
+    def outward(step, carry):
+        d = 4 + (1 - 2 * (step % 2)) * ((step + 1) // 2)
+        d = 8 - d
+        collect((z + d) % 8)
+        z_copy(d).start()
+        return carry
+
+    lax.fori_loop(0, 7, outward, 0)
+    collect(z)
+    each(8, z_wait)
+    total = part_ref[z]
+    for d in range(1, 8):
+        total = total + got_ref[(z + d) % 8]
+    sum_ref[...] = total
+
+    def block(d):
+        return pl.ds(pl.multiple_of(8 * d, 8), 8)
+
+    def plane_copy(d):
+        peer = (own + STEP32 * d) % 32
+        return remote(sum_ref.at[block(peer)], out_ref.at[block(own)], sendp.at[d], recvp.at[own], place_of(peer, z))
+
+    def plane_wait(d):
+        peer = (own + STEP32 * d) % 32
+        remote(sum_ref.at[block(peer)], out_ref.at[block(peer)], sendp.at[d], recvp.at[peer], place_of(peer, z)).wait_recv()
+
+    each(32, lambda d: plane_copy(d).start())
+    out_ref[block(own), :] = sum_ref[block(own), :]
+    each(32, plane_wait)
+    each(8, lambda d: z_copy(d).wait_send())
+    each(32, lambda d: plane_copy(d).wait_send())
 
 
 def scatter_kernel(idx_ref, c_ref, tw_ref, m_ref, m1_ref, w4_ref, f_ref, out_ref, w_ref, full_ref, l_ref, crep_ref, z0_ref, z1_ref):
@@ -382,10 +439,10 @@
         crep_ref[at] = spread[:, 128 * at : 128 * at + 128]
 
     def clear(step, carry):
-        tus = pl.ds(pl.multiple_of(step * 16, 16), 16)
-        zero = jnp.zeros((16, 16, 8, 128), F32)
-        z0_ref[:, tus] = zero
-        z1_ref[:, tus] = zero
+        spots = pl.ds(pl.multiple_of(step * 128, 128), 128)
+        zero = jnp.zeros((2, 128, 8, 128), F32)
+        z0_ref[:, spots] = zero
+        z1_ref[:, spots] = zero
         return carry
 
     lax.fori_loop(0, 16, clear, 0)
@@ -395,23 +452,22 @@
             z_ref = (z0_ref, z1_ref)[k % 2]
             half, row = k // 8, k % 8
             word = idx_ref[it % 32, 0, it // 32 * 16 + k]
-            tu, tv = word & 255, word >> 8
-            t = (tv >> 2) & 7
+            spot, tv = word & 2047, word >> 11
             cr = jnp.broadcast_to(crep_ref[2 * half, pl.ds(it * 8 + row, 1), :], (8, 128))
             ci = jnp.broadcast_to(crep_ref[2 * half + 1, pl.ds(it * 8 + row, 1), :], (8, 128))
             wr, wi = w_ref[tv, 0], w_ref[tv, 1]
-            z_ref[t, tu] += cr * wr + ci * wi
-            z_ref[8 + t, tu] += ci * wr - cr * wi
+            z_ref[0, spot] += cr * wr + ci * wi
+            z_ref[1, spot] += ci * wr - cr * wi
         return carry
 
     lax.fori_loop(0, 256, add, 0)
 
     def stage(step, carry):
-        tus = pl.ds(pl.multiple_of(step * 32, 32), 32)
         res = None
         for block in range(8):
             lanes = slice(256 * block, 256 * block + 256)
-            parts = [(z0_ref[t, tus] + z1_ref[t, tus]).reshape(256, 128) for t in (2 * block, 2 * block + 1)]
+            spots = [pl.ds(pl.multiple_of(t % 8 * 256 + step * 32, 32), 32) for t in (2 * block, 2 * block + 1)]
+            parts = [(z0_ref[block // 4, at] + z1_ref[block // 4, at]).reshape(256, 128) for at in spots]
             left = halves(jnp.concatenate(parts, axis=1))
             part = dot3(left, (full_ref[0, :, lanes], full_ref[1, :, lanes]), dot_t)
             res = part if res is None else res + part
@@ -487,11 +543,11 @@
         return pl.ds(pl.multiple_of(8 * d, 8), 8)
 
     def plane_copy(d):
-        peer = (own + d) % 32
+        peer = (own + STEP32 * d) % 32
         return remote(out_ref.at[block(peer)], g_ref.at[z, block(own)], send1.at[d], recv1.at[own], place_of(peer, z))
 
     def plane_wait(d):
-        peer = (own + d) % 32
+        peer = (own + STEP32 * d) % 32
         remote(out_ref.at[block(peer)], g_ref.at[z, block(peer)], send1.at[d], recv1.at[peer], place_of(peer, z)).wait_recv()
 
     each(32, lambda d: plane_copy(d).start())
@@ -577,7 +633,8 @@
 
 def per_device(model_image, vis_coords, vis_observed, tile_slot, tile_group, w_plane, vis_count):
     slab, z, x = (lax.axis_index(a) for a in SLAB_BL)
-    word = tile_slot + 256 * (32 * slab + tile_group[:, 0])
+    tv = 32 * slab + tile_group[:, 0]
+    word = tile_slot + 256 * ((tv >> 2) & 7) + 2048 * tv
     lane = jnp.arange(128, dtype=jnp.int32)
     word_row = jnp.where(lane // 16 == z, jnp.tile(word, 8), 0).reshape(1, 128)
     own = slab * 4 + x
@@ -592,7 +649,8 @@
     same = (half[:, None] == n_half[None, :]) & (jj[:, None] == n_jj[None, :])
     pick = jnp.where(part[:, None] == n_part[None, :], phz[0][:, None], jnp.where(part[:, None] == 0, -phz[1][:, None], phz[1][:, None]))
     spread = jnp.where(same, pick, 0.0)
-    spread = jnp.stack(halves(spread))
+    high = lax.reduce_precision(spread, 8, 7)
+    spread = jnp.stack([high.astype(BF16), (spread - high).astype(BF16)])
     pa, pb = phases(vis_coords[:, 0, :]), phases(vis_coords[:, 1, :])
     mm = (jnp.arange(SUB, dtype=jnp.int32) - SUB // 2).astype(F32)
     radius = (mm[:, None] ** 2 + mm[None, :] ** 2) / (SUB // 2) ** 2
@@ -613,10 +671,10 @@
             pltpu.VMEM((8, 1, 128), jnp.int32),
             pltpu.VMEM((1, 128), jnp.int32),
             DMA,
-            DMA((4, 8)),
-            DMA((4, 8)),
-            DMA((4, 32)),
-            DMA((4, 32)),
+            DMA((CHUNKS, 8)),
+            DMA((CHUNKS, 8)),
+            DMA((CHUNKS, 32)),
+            DMA((CHUNKS, 32)),
             DMA((8,)),
             DMA((8,)),
             DMA((32,)),
@@ -625,20 +683,27 @@
         collective_id=0,
     )(model_image.reshape(2, 4, 8, 32, 256), word_row)
     a = a.reshape(8, 4, 2, 32, 256)
-    partial = call(
+    tiles = call(
         gather_kernel,
-        f32(2048, 128),
+        f32(256, 128),
         [SMEM] + in_vmem(6),
         [
             pltpu.VMEM((256, 2, 8, 128), F32),
             pltpu.VMEM((2, 256, 2048), BF16),
             pltpu.VMEM((2, 2048, 128), F32),
             pltpu.VMEM((2, 2048, 128), F32),
-            pltpu.VMEM((16, 256, 8, 128), F32),
+            pltpu.VMEM((2, 2048, 8, 128), F32),
+            pltpu.VMEM((4, 256, 128), F32),
+            pltpu.VMEM((8, 256, 128), F32),
+            pltpu.VMEM((8, 256, 128), F32),
+            pltpu.VMEM((256, 128), F32),
+            DMA((8,)),
+            DMA((8,)),
+            DMA((32,)),
+            DMA((32,)),
         ],
-    )(words, a, tw, rows, columns, screens, phz)
-    summed = lax.psum_scatter(partial.reshape(8, 256, 128), "bl_0", scatter_dimension=0, tiled=True)
-    tiles = lax.all_to_all(summed.reshape(32, 8, 128), PLANE, split_axis=0, concat_axis=0, tiled=True)
+        collective_id=3,
+    )(words, a, tw, rows, columns, screens, spread)
     vis, every = call(
         subgrid_kernel,
         (f32(32, 128), f32(8, 256, 128)),
@@ -646,7 +711,7 @@
         [pltpu.VMEM((256, 128), F32), DMA((32,)), DMA((32,)), DMA((4, 4)), DMA((4, 4)), DMA((3, 4)), DMA((3, 4))],
         collective_id=1,
     )(
-        tiles.reshape(256, 128), right, left, wa, wb, pa, pb, vis_observed.reshape(32, 128), live
+        tiles, right, left, wa, wb, pa, pb, vis_observed.reshape(32, 128), live
     )
     every = every.reshape(2048, 128)
     spots = call(
@@ -658,8 +723,8 @@
             pltpu.VMEM((2, 256, 2048), BF16),
             pltpu.VMEM((2, 2048, 128), F32),
             pltpu.VMEM((4, 2048, 128), F32),
-            pltpu.VMEM((16, 256, 8, 128), F32),
-            pltpu.VMEM((16, 256, 8, 128), F32),
+            pltpu.VMEM((2, 2048, 8, 128), F32),
+            pltpu.VMEM((2, 2048, 8, 128), F32),
         ],
     )(words, every, tw, rows, columns, screens, spread)
     image = call(
@@ -670,11 +735,11 @@
             pltpu.VMEM((32, 2, 32, 256), F32),
             pltpu.VMEM((8, 2, 4, 32, 256), F32),
             DMA,
-            DMA((4,)),
-            DMA((4, 32)),
-            DMA((4, 32)),
-            DMA((4, 8)),
-            DMA((4, 8)),
+            DMA((CHUNKS,)),
+            DMA((CHUNKS, 32)),
+            DMA((CHUNKS, 32)),
+            DMA((CHUNKS, 8)),
+            DMA((CHUNKS, 8)),
         ],
         collective_id=2,
         out_specs=ANY,

time: 345 us -> 266 us (0.77)
  waiting for transfers between devices: 29.8 us -> 0 us
  Pallas kernels: 274 us -> 249 us
  between operations: 14.2 us -> 0.77 us
  starting transfers between devices: 12.5 us -> 0 us
    reduce_scatter x1 -> x0, waiting for transfers between devices: 23.7 us -> none  [per_device(): lax.psum_scatter(partial.reshape(8, 256, 128), 'bl_0', scatter_dimension=...]
    pallas_call x1, Pallas kernels: 75.3 us -> 59.4 us  [per_device(): call(gather_kernel, f32(256, 128), [SMEM] + in_vmem(6), [pltpu.VMEM((256,...]
    all_to_all x1 -> x0, starting transfers between devices: 12.5 us -> none  [per_device(): lax.all_to_all(summed.reshape(32, 8, 128), PLANE, split_axis=0, concat_ax...]
    all_to_all x1 -> x0, waiting for transfers between devices: 6.05 us -> none  [per_device(): lax.all_to_all(summed.reshape(32, 8, 128), PLANE, split_axis=0, concat_ax...]
    pallas_call x1, Pallas kernels: 42.1 us -> 38.1 us  [per_device(): call(scatter_kernel, f32(8, 4, 2, 32, 256), [SMEM] + in_vmem(6), [pltpu.V...]
  transfers between devices with their start and end apart: 2 -> 0, of which waited for: 2 -> 0; matrix products, arithmetic and copies ran while one was open for 2% -> 0% of each run, Pallas kernels for 0% -> 0%
where the time goes in v2:
time: 266 us; the launch traced here: 265 us
  Pallas kernels  249 us (94%)
  other arithmetic  10.8 us (4%)
  local copies, waits for them, and re-layouts  4.62 us (2%)
    pallas_call x1, Pallas kernels, per_device(): call(forward_kernel, (f32(32, 2, 32, 256), jax.ShapeDtypeStruct((32, 1, 1...  63.4 us
    pallas_call x1, Pallas kernels, per_device(): call(gather_kernel, f32(256, 128), [SMEM] + in_vmem(6), [pltpu.VMEM((256,...  59.4 us
    pallas_call x1, Pallas kernels, per_device(): call(backward_kernel, f32(2, 4, 8, 32, 256), [ANY], [pltpu.VMEM((32, 2, 3...  54.3 us
    pallas_call x1, Pallas kernels, per_device(): call(scatter_kernel, f32(8, 4, 2, 32, 256), [SMEM] + in_vmem(6), [pltpu.V...  38.1 us
    pallas_call x1, Pallas kernels, per_device(): call(subgrid_kernel, (f32(32, 128), f32(8, 256, 128)), in_vmem(9), [pltpu...  33.8 us

profile of v2, /device:TPU:1, one launch (start us, length us, event | category | flops | bytes accessed | tf_op | source)
XLA Modules:
  0.0 265.2 jit_solution(13747768657403222451)
XLA Ops:
  0.6 0.7 bitcast_add_fusion
  1.3 0.7 convert_multiply_fusion.1
  2.0 0.1 sine_negate_fusion.1
  2.1 0.1 sine_negate_fusion
  2.2 0.1 tile.10
  2.3 0.6 compare_select_fusion.5.word_ref
  2.9 1.3 fusion.1.live_ref
  4.2 0.1 add_multiply_fusion
  4.3 0.8 slice_multiply_fusion
  5.1 0.2 reduce-precision_convert_fusion
  5.3 0.8 pad_maximum_fusion.2.f_ref
  6.0 0.8 broadcast_in_dim.17.tw_ref
  6.9 1.0 multiply_sine_fusion.2
  7.9 0.8 pad_maximum_fusion.4.wb_ref
  8.7 0.8 pad_maximum_fusion.3.wa_ref
  9.5 1.9 multiply_cosine_fusion
  11.4 1.1 pad_maximum_fusion
  12.5 63.4 %shard_map.131 = (f32[32,2,32,256]{3,2,1,0:T(8,128)}, s32[32,1,128]{2,1,0:T(1,128)}) custom-call(f32[2,4,8,32,256]{4,3,2,1,0:T(8,128)} %bitcast.22, s32[1,128]{1,0:T(1,128)} %compare_select_fusion.5.word_ref), custom_call_target="tpu_custom_call" | custom-call | tf_op jit(solution)/shard_map/pallas_call | solution.py:664
  75.9 59.4 %shard_map.132.t_ref = f32[256,128]{1,0:T(8,128)} custom-call(s32[32,1,128]{2,1,0:T(1,128)} %get-tuple-element.6.idx_ref, f32[8,4,2,32,256]{4,3,2,1,0:T(8,128)} %bitcast.21, f32[2,256,128]{2,1,0:T(8,128)} %broadcast_in_dim.17.tw_ref, bf16[4,256,256]{2,1,0:T(8,128)(2,1)} %constant.171.clone.m_ref, bf16[4,128,1024]{2,1,0:T(8,128)(2,1)} %constant.172.clone.m1_ref, ...), custom_call_target="tpu_custom_call" | custom-call | tf_op jit(solution)/shard_map/pallas_call | solution.py:686
  135.3 33.8 %shard_map.133 = (f32[32,128]{1,0:T(8,128)}, f32[8,256,128]{2,1,0:T(8,128)}) custom-call(f32[256,128]{1,0:T(8,128)} %shard_map.132.t_ref, f32[128,256]{1,0:T(8,128)} %constant.174.clone.right_ref, f32[2,32,64]{2,1,0:T(8,128)} %constant.175.clone.left_ref, f32[8,32,128]{2,1,0:T(8,128)} %pad_maximum_fusion.3.wa_ref, f32[8,32,128]{2,1,0:T(8,128)} %pad_maximum_fusion.4.wb_ref, ...), custom_call_target="tpu_custom_call" | custom-call | tf_op jit(solution)/shard_map/pallas_call | solution.py:707
  169.0 38.1 %shard_map.134 = f32[8,4,2,32,256]{4,3,2,1,0:T(8,128)} custom-call(s32[32,1,128]{2,1,0:T(1,128)} %get-tuple-element.6.idx_ref, f32[2048,128]{1,0:T(8,128)} %bitcast.23, f32[2,256,128]{2,1,0:T(8,128)} %broadcast_in_dim.17.tw_ref, bf16[4,256,256]{2,1,0:T(8,128)(2,1)} %constant.171.clone.m_ref, bf16[4,128,1024]{2,1,0:T(8,128)(2,1)} %constant.172.clone.m1_ref, ...), custom_call_target="tpu_custom_call" | custom-call | tf_op jit(solution)/shard_map/pallas_call | solution.py:717
  207.2 54.3 %shard_map.135 = f32[2,4,8,32,256]{4,3,2,1,0:T(8,128)} custom-call(f32[32,2,32,256]{3,2,1,0:T(8,128)} %bitcast.20), custom_call_target="tpu_custom_call" | custom-call | tf_op jit(solution)/shard_map/pallas_call | solution.py:730
  261.5 0.0 copy-start
  261.5 3.0 %copy.16 = f32[2,1024,256]{2,1,0:T(8,128)} copy(f32[2,1024,256]{2,1,0:T(8,128)} %bitcast.19) | data formatting | bytes 4194304
  264.6 0.0 copy-done
  264.6 0.6 copy.17
  (12 shorter events, 0.1 us)
Async XLA Ops:
  261.5 3.1 %copy-start = (f32[32,128]{1,0:T(8,128)S(1)}, f32[32,128]{1,0:T(8,128)}, u32[]{:S(2)}) copy-start(f32[32,128]{1,0:T(8,128)} %get-tuple-element.9) | copy-start | bytes 49156

commit v3 on v2

--- a/solution.py
+++ b/solution.py
@@ -22,7 +22,6 @@
 MESH = pl.DeviceIdType.MESH
 ANY = pl.BlockSpec(memory_space=pl.ANY)
 DMA = pltpu.SemaphoreType.DMA
-VMEM_LIMIT = 62 * 1024 * 1024
 
 
 def unit(numerator, modulus):
@@ -179,7 +178,47 @@
     return pl.ds(32 // CHUNKS * c, 32 // CHUNKS)
 
 
-def forward_kernel(image_ref, word_ref, a_ref, idx_ref, v_ref, w_ref, zrow_ref, row_ref, local, send1, recv1, send2, recv2, sendz, recvz, sendi, recvi):
+def device_tables(slab, z, own, coord_ref, plane_ref, count_ref, pa_ref, pb_ref, wa_ref, wb_ref, live_ref, tw_ref, f_ref):
+    def iota(shape, dim):
+        return lax.broadcasted_iota(jnp.int32, shape, dim)
+
+    offsets = (iota((SUB, 128), 0) - SUB // 2).astype(F32)
+
+    def subgrid_phases(g, carry):
+        for at, out_ref in enumerate((pa_ref, pb_ref)):
+            along = (-2.0 * math.pi / SUB) * coord_ref[pl.ds(2 * g + at, 1), :] * offsets
+            out_ref[0, g], out_ref[1, g] = jnp.cos(along), jnp.sin(along)
+        live_ref[pl.ds(g, 1), :] = jnp.where(iota((1, 128), 1) < count_ref[g], 1.0, 0.0)
+        return carry
+
+    lax.fori_loop(0, 16, subgrid_phases, 0)
+    lane = iota((SUB, 128), 1)
+    across = (lane % SUB - SUB // 2).astype(F32)
+    radius = (offsets * offsets + across * across) * (1.0 / (SUB // 2) ** 2)
+
+    def screens(k, carry):
+        plane = jnp.where(lane < 64, plane_ref[k].astype(F32), plane_ref[k + 8].astype(F32))
+        phase = -W_STEP * plane * radius
+        wa_ref[k], wb_ref[k] = jnp.cos(phase), jnp.sin(phase)
+        return carry
+
+    lax.fori_loop(0, 8, screens, 0)
+    angle = (2.0 * math.pi / N) * (own * iota((256, 128), 0)).astype(F32)
+    tw_ref[0], tw_ref[1] = jnp.cos(angle), -jnp.sin(angle)
+    source, target = iota((128, 512), 0), iota((128, 512), 1)
+    same = (source // 64 == target // 256) & (source % 32 == target % 32)
+    part, n_part = source // 32 % 2, target // 128 % 2
+    shift = (2.0 * math.pi / 8.0) * (target % 32 * z % 8).astype(F32)
+    cos, sin = jnp.cos(shift) * (1.0 / N), jnp.sin(shift) * (1.0 / N)
+    value = jnp.where(part == n_part, cos, jnp.where(part == 0, sin, -sin))
+    f_ref[0], f_ref[1] = halves(jnp.where(same, value, 0.0))
+
+
+def forward_kernel(
+    slot_ref, group_ref, plane_ref, count_ref, image_ref, coord_ref,
+    a_ref, idx_ref, pa_ref, pb_ref, wa_ref, wb_ref, live_ref, tw_ref, f_ref,
+    word_ref, v_ref, w_ref, zrow_ref, row_ref, local, send1, recv1, send2, recv2, sendz, recvz, sendi, recvi,
+):
     slab, z, x, own = greet(True, True)
 
     def word_copy(d):
@@ -205,11 +244,19 @@
     def row_copy(d):
         return remote(row_ref, idx_ref.at[own], sendi.at[d], recvi.at[own], place_of((own + d) % 32, z))
 
-    each(8, lambda d: word_copy(d).start())
+    lane = lax.broadcasted_iota(jnp.int32, (1, 128), 1)
+    words = jnp.zeros((1, 128), jnp.int32)
+    for k in range(16):
+        tv = 32 * slab + group_ref[k]
+        word = slot_ref[k] + 256 * ((tv >> 2) & 7) + 2048 * tv
+        words = jnp.where(lane == 16 * z + k, word, words)
+    word_ref[...] = words
     mine = pltpu.make_async_copy(image_ref.at[:, :, slab], v_ref.at[slab], local)
     mine.start()
     for c in range(CHUNKS):
         each(8, lambda d: slab_copy(c, d).start())
+    each(8, lambda d: word_copy(d).start())
+    device_tables(slab, z, own, coord_ref, plane_ref, count_ref, pa_ref, pb_ref, wa_ref, wb_ref, live_ref, tw_ref, f_ref)
 
     def word_wait(d):
         peer = (z + d) % 8
@@ -258,11 +305,11 @@
 
     def slab_copy(c, d):
         peer = (slab + STEP8 * d) % 8
-        return remote(v_ref.at[peer, :, :, chunk(c)], out_ref.at[:, :, slab, chunk(c)], send2.at[c, d], recv2.at[c, slab], (peer, z, x))
+        return remote(v_ref.at[peer, :, :, chunk(c)], out_ref.at[slab, :, :, chunk(c)], send2.at[c, d], recv2.at[c, slab], (peer, z, x))
 
     def slab_wait(c, d):
         peer = (slab + STEP8 * d) % 8
-        remote(v_ref.at[peer, :, :, chunk(c)], out_ref.at[:, :, peer, chunk(c)], send2.at[c, d], recv2.at[c, peer], (peer, z, x)).wait_recv()
+        remote(v_ref.at[peer, :, :, chunk(c)], out_ref.at[peer, :, :, chunk(c)], send2.at[c, d], recv2.at[c, peer], (peer, z, x)).wait_recv()
 
     mine = pltpu.make_async_copy(spot_ref.at[own], w_ref.at[own], local)
     mine.start()
@@ -274,7 +321,7 @@
         each(32, lambda d: plane_wait(c, d))
         unbutterfly(w_ref, v_ref, c)
         each(8, lambda d: slab_copy(c, d).start())
-        copy = pltpu.make_async_copy(v_ref.at[slab, :, :, chunk(c)], out_ref.at[:, :, slab, chunk(c)], keep.at[c])
+        copy = pltpu.make_async_copy(v_ref.at[slab, :, :, chunk(c)], out_ref.at[slab, :, :, chunk(c)], keep.at[c])
         copy.start()
         kept.append(copy)
     for c in range(CHUNKS):
@@ -330,7 +377,7 @@
 
 def gather_kernel(
     idx_ref, a_ref, tw_ref, m_ref, m1_ref, w4_ref, f_ref, out_ref,
-    w_ref, full_ref, high_ref, low_ref, z_ref, s_ref, part_ref, got_ref, sum_ref, sendz, recvz, sendp, recvp,
+    w_ref, full_ref, high_ref, low_ref, z_ref, s_ref, part_ref, right_ref, left_ref, sum_ref, sendr, recvr, sendl, recvl, sendp, recvp,
 ):
     slab, z, x, own = greet(True, True)
     spread_screens(w4_ref, w_ref)
@@ -390,27 +437,48 @@
         sums = jnp.concatenate([s_ref[at] for at in range(4)], axis=1)
         part_ref[zc] = dot3(halves(sums), (f_ref[0], f_ref[1]), dot_t)
 
-    def z_copy(d):
-        peer = (z + d) % 8
-        return remote(part_ref.at[peer], got_ref.at[z], sendz.at[d], recvz.at[z], (slab, peer, x))
-
-    def z_wait(d):
-        peer = (z + d) % 8
-        remote(part_ref.at[peer], got_ref.at[peer], sendz.at[d], recvz.at[peer], (slab, peer, x)).wait_recv()
+    def half_of(ref, u):
+        return ref.at[pl.ds(128 * u, 128)]
+
+    def right_copy(h, u):
+        src, dst = half_of(part_ref.at[(z + 4 - h) % 8], u), half_of(right_ref.at[h], u)
+        return remote(src, dst, sendr.at[h, u], recvr.at[h, u], (slab, (z + 1) % 8, x))
+
+    def left_copy(h, u):
+        src, dst = half_of(part_ref.at[(z + 5 + h) % 8], u), half_of(left_ref.at[h], u)
+        return remote(src, dst, sendl.at[h, u], recvl.at[h, u], (slab, (z + 7) % 8, x))
+
+    def pass_on(zc, h, copy, held_ref):
+        for u in range(2):
+            rows = pl.ds(128 * u, 128)
+
+            @pl.when(h > 0)
+            def _():
+                copy(jnp.maximum(h - 1, 0), u).wait_recv()
+                part_ref[zc, rows, :] += held_ref[jnp.maximum(h - 1, 0), rows, :]
+
+            copy(h, u).start()
 
     def outward(step, carry):
-        d = 4 + (1 - 2 * (step % 2)) * ((step + 1) // 2)
-        d = 8 - d
-        collect((z + d) % 8)
-        z_copy(d).start()
-        return carry
-
-    lax.fori_loop(0, 7, outward, 0)
-    collect(z)
-    each(8, z_wait)
-    total = part_ref[z]
-    for d in range(1, 8):
-        total = total + got_ref[(z + d) % 8]
+        h, odd = step // 2, step % 2
+        zc = (z + (1 - odd) * (4 - h) + odd * (5 + h)) % 8
+        collect(zc)
+
+        @pl.when(odd == 0)
+        def _():
+            pass_on(zc, h, right_copy, right_ref)
+
+        @pl.when((odd == 1) & (step < 7))
+        def _():
+            pass_on(zc, h, left_copy, left_ref)
+
+        return carry
+
+    lax.fori_loop(0, 8, outward, 0)
+    for u in range(2):
+        left_copy(2, u).wait_recv()
+        right_copy(3, u).wait_recv()
+    total = part_ref[z] + (right_ref[3] + left_ref[2])
     sum_ref[...] = total
 
     def block(d):
@@ -427,7 +495,11 @@
     each(32, lambda d: plane_copy(d).start())
     out_ref[block(own), :] = sum_ref[block(own), :]
     each(32, plane_wait)
-    each(8, lambda d: z_copy(d).wait_send())
+    for u in range(2):
+        for h in range(4):
+            right_copy(h, u).wait_send()
+            if h < 3:
+                left_copy(h, u).wait_send()
     each(32, lambda d: plane_copy(d).wait_send())
 
 
@@ -601,17 +673,11 @@
     return right.astype(np.float32), (left / (SUB * SUB)).astype(np.float32)
 
 
-def phases(coords):
-    offsets = (jnp.arange(SUB, dtype=jnp.int32) - SUB // 2).astype(F32)
-    along = (-2.0 * math.pi / SUB) * coords[:, None, :] * offsets[None, :, None]
-    return jnp.stack([jnp.cos(along), jnp.sin(along)])
-
-
 def in_vmem(count):
     return [pl.BlockSpec(memory_space=pltpu.VMEM)] * count
 
 
-def call(kernel, out, specs, scratch=(), collective_id=None, out_specs=None):
+def call(kernel, out, specs, scratch=(), collective_id=None, out_specs=None, vmem=62):
     return pl.pallas_call(
         kernel,
         out_shape=out,
@@ -619,7 +685,7 @@
         out_specs=out_specs or jax.tree.map(lambda _: pl.BlockSpec(memory_space=pltpu.VMEM), out),
         scratch_shapes=list(scratch),
         compiler_params=pltpu.CompilerParams(
-            vmem_limit_bytes=VMEM_LIMIT, collective_id=collective_id, has_side_effects=collective_id is not None
+            vmem_limit_bytes=vmem * 1024 * 1024, collective_id=collective_id, has_side_effects=collective_id is not None
         ),
     )
 
@@ -632,40 +698,25 @@
 
 
 def per_device(model_image, vis_coords, vis_observed, tile_slot, tile_group, w_plane, vis_count):
-    slab, z, x = (lax.axis_index(a) for a in SLAB_BL)
-    tv = 32 * slab + tile_group[:, 0]
-    word = tile_slot + 256 * ((tv >> 2) & 7) + 2048 * tv
-    lane = jnp.arange(128, dtype=jnp.int32)
-    word_row = jnp.where(lane // 16 == z, jnp.tile(word, 8), 0).reshape(1, 128)
-    own = slab * 4 + x
-    angle = (2.0 * math.pi / N) * (own * jnp.arange(256, dtype=jnp.int32)).astype(F32)
-    tw = jnp.broadcast_to(jnp.stack([jnp.cos(angle), -jnp.sin(angle)])[:, :, None], (2, 256, 128))
-    j = jnp.arange(128, dtype=jnp.int32)
-    shift = (2.0 * math.pi / 8.0) * (j * z % 8).astype(F32)
-    phz = jnp.stack([jnp.cos(shift), -jnp.sin(shift)]) / N
-    half, part, jj = j // 64, j // 32 % 2, j % 32
-    n = jnp.arange(512, dtype=jnp.int32)
-    n_half, n_part, n_jj = n // 256, n // 128 % 2, n % 32
-    same = (half[:, None] == n_half[None, :]) & (jj[:, None] == n_jj[None, :])
-    pick = jnp.where(part[:, None] == n_part[None, :], phz[0][:, None], jnp.where(part[:, None] == 0, -phz[1][:, None], phz[1][:, None]))
-    spread = jnp.where(same, pick, 0.0)
-    high = lax.reduce_precision(spread, 8, 7)
-    spread = jnp.stack([high.astype(BF16), (spread - high).astype(BF16)])
-    pa, pb = phases(vis_coords[:, 0, :]), phases(vis_coords[:, 1, :])
-    mm = (jnp.arange(SUB, dtype=jnp.int32) - SUB // 2).astype(F32)
-    radius = (mm[:, None] ** 2 + mm[None, :] ** 2) / (SUB // 2) ** 2
-    turned = -W_STEP * w_plane.astype(F32)[:, None, None] * radius[None]
-    lanes = lambda value: jnp.concatenate([value[:8], value[:8], value[8:], value[8:]], axis=2)
-    wa, wb = lanes(jnp.cos(turned)), lanes(jnp.sin(turned))
-    live = (jnp.arange(128, dtype=jnp.int32)[None, :] < vis_count[:, None]).astype(F32)
     rows, columns, screens = row_tables(), column_tables(), screen_tables()
     right, left = subgrid_tables()
 
-    a, words = call(
+    a, words, pa, pb, wa, wb, live, tw, spread = call(
         forward_kernel,
-        (f32(32, 2, 32, 256), jax.ShapeDtypeStruct((32, 1, 128), jnp.int32)),
-        [ANY] + in_vmem(1),
+        (
+            f32(32, 2, 32, 256),
+            jax.ShapeDtypeStruct((32, 1, 128), jnp.int32),
+            f32(2, 16, 32, 128),
+            f32(2, 16, 32, 128),
+            f32(8, 32, 128),
+            f32(8, 32, 128),
+            f32(16, 128),
+            f32(2, 256, 128),
+            jax.ShapeDtypeStruct((2, 128, 512), BF16),
+        ),
+        [SMEM] * 4 + [ANY] + in_vmem(1),
         [
+            pltpu.VMEM((1, 128), jnp.int32),
             pltpu.VMEM((8, 2, 4, 32, 256), F32),
             pltpu.VMEM((32, 2, 32, 256), F32),
             pltpu.VMEM((8, 1, 128), jnp.int32),
@@ -681,7 +732,7 @@
             DMA((32,)),
         ],
         collective_id=0,
-    )(model_image.reshape(2, 4, 8, 32, 256), word_row)
+    )(tile_slot, tile_group[:, 0], w_plane, vis_count, model_image.reshape(2, 4, 8, 32, 256), vis_coords.reshape(32, 128))
     a = a.reshape(8, 4, 2, 32, 256)
     tiles = call(
         gather_kernel,
@@ -695,10 +746,13 @@
             pltpu.VMEM((2, 2048, 8, 128), F32),
             pltpu.VMEM((4, 256, 128), F32),
             pltpu.VMEM((8, 256, 128), F32),
-            pltpu.VMEM((8, 256, 128), F32),
+            pltpu.VMEM((4, 256, 128), F32),
+            pltpu.VMEM((3, 256, 128), F32),
             pltpu.VMEM((256, 128), F32),
-            DMA((8,)),
-            DMA((8,)),
+            DMA((4, 2)),
+            DMA((4, 2)),
+            DMA((3, 2)),
+            DMA((3, 2)),
             DMA((32,)),
             DMA((32,)),
         ],
@@ -729,7 +783,7 @@
     )(words, every, tw, rows, columns, screens, spread)
     image = call(
         backward_kernel,
-        f32(2, 4, 8, 32, 256),
+        f32(8, 2, 4, 32, 256),
         [ANY],
         [
             pltpu.VMEM((32, 2, 32, 256), F32),
@@ -743,7 +797,9 @@
         ],
         collective_id=2,
         out_specs=ANY,
-    )(spots.reshape(32, 2, 32, 256)).reshape(2, 1024, 256)
+        vmem=16,
+    )(spots.reshape(32, 2, 32, 256))
+    image = image.transpose(1, 2, 0, 3, 4).reshape(2, 1024, 256)
     return image, vis.reshape(16, 2, 128)
 
 

time: 266 us -> 249 us (0.936)
  other arithmetic: 10.8 us -> 0 us
  Pallas kernels: 249 us -> 245 us
    pallas_call x1, Pallas kernels: 59.4 us -> 54.4 us  [per_device(): call(gather_kernel, f32(256, 128), [SMEM] + in_vmem(6), [pltpu.VMEM((256,...]
where the time goes in v3:
time: 249 us
  Pallas kernels  245 us (98%)
  local copies, waits for them, and re-layouts  3.66 us (1%)
    pallas_call x1, Pallas kernels, per_device(): call(forward_kernel, (f32(32, 2, 32, 256), jax.ShapeDtypeStruct((32, 1, 1...  64.6 us
    pallas_call x1, Pallas kernels, per_device(): call(backward_kernel, f32(8, 2, 4, 32, 256), [ANY], [pltpu.VMEM((32, 2, 3...  55 us
    pallas_call x1, Pallas kernels, per_device(): call(gather_kernel, f32(256, 128), [SMEM] + in_vmem(6), [pltpu.VMEM((256,...  54.4 us
    pallas_call x1, Pallas kernels, per_device(): call(scatter_kernel, f32(8, 4, 2, 32, 256), [SMEM] + in_vmem(6), [pltpu.V...  38.1 us
    pallas_call x1, Pallas kernels, per_device(): call(subgrid_kernel, (f32(32, 128), f32(8, 256, 128)), in_vmem(9), [pltpu...  32.6 us

profile of v3, /device:TPU:1, one launch (start us, length us, event | category | flops | bytes accessed | tf_op | source)
XLA Modules:
  0.0 249.1 jit_solution(16717217010503679808)
XLA Ops:
  0.6 64.6 %shard_map.131 = (f32[32,2,32,256]{3,2,1,0:T(8,128)}, s32[32,1,128]{2,1,0:T(1,128)}, f32[2,16,32,128]{3,2,1,0:T(8,128)}, f32[2,16,32,128]{3,2,1,0:T(8,128)}, f32...) custom-call(s32[16]{0:T(128)} %slot_ref.1, ...), custom_call_target="tpu_custom_call" | custom-call | tf_op jit(solution)/shard_map/pallas_call | solution.py:704
  65.3 54.4 %shard_map.132.t_ref = f32[256,128]{1,0:T(8,128)} custom-call(s32[32,1,128]{2,1,0:T(1,128)} %get-tuple-element.13.idx_ref, f32[8,4,2,32,256]{4,3,2,1,0:T(8,128)} %bitcast.12, f32[2,256,128]{2,1,0:T(8,128)} %get-tuple-element.15.tw_ref, bf16[4,256,256]{2,1,0:T(8,128)(2,1)} %constant.10.clone.m_ref, bf16[4,128,1024]{2,1,0:T(8,128)(2,1)} %constant.11.clone.m1_ref, ...), custom_call_target="tpu_custom_call" | custom-call | tf_op jit(solution)/shard_map/pallas_call | solution.py:737
  119.7 32.6 %shard_map.133 = (f32[32,128]{1,0:T(8,128)}, f32[8,256,128]{2,1,0:T(8,128)}) custom-call(f32[256,128]{1,0:T(8,128)} %shard_map.132.t_ref, f32[128,256]{1,0:T(8,128)} %constant.13.clone.right_ref, f32[2,32,64]{2,1,0:T(8,128)} %constant.14.clone.left_ref, f32[8,32,128]{2,1,0:T(8,128)} %get-tuple-element.17.wa_ref, f32[8,32,128]{2,1,0:T(8,128)} %get-tuple-element.18.wb_ref, ...), custom_call_target="tpu_custom_call" | custom-call | tf_op jit(solution)/shard_map/pallas_call | solution.py:761
  152.4 38.1 %shard_map.134 = f32[8,4,2,32,256]{4,3,2,1,0:T(8,128)} custom-call(s32[32,1,128]{2,1,0:T(1,128)} %get-tuple-element.13.idx_ref, f32[2048,128]{1,0:T(8,128)} %bitcast.15, f32[2,256,128]{2,1,0:T(8,128)} %get-tuple-element.15.tw_ref, bf16[4,256,256]{2,1,0:T(8,128)(2,1)} %constant.10.clone.m_ref, bf16[4,128,1024]{2,1,0:T(8,128)(2,1)} %constant.11.clone.m1_ref, ...), custom_call_target="tpu_custom_call" | custom-call | tf_op jit(solution)/shard_map/pallas_call | solution.py:771
  190.5 0.0 copy-start
  190.5 1.6 copy-done
  192.0 55.0 %shard_map.135 = f32[8,2,4,32,256]{4,3,2,1,0:T(8,128)S(1)} custom-call(f32[32,2,32,256]{3,2,1,0:T(8,128)S(1)} %bitcast.11), custom_call_target="tpu_custom_call" | custom-call | tf_op jit(solution)/shard_map/pallas_call | solution.py:784
  247.0 0.0 copy-start.1
  247.1 1.5 copy.14
  248.5 0.0 copy-done.1
  248.5 0.6 copy.16
Async XLA Ops:
  190.5 1.6 copy-start
  247.0 1.5 copy-start.1

commit v4 on v3

--- a/solution.py
+++ b/solution.py
@@ -212,84 +212,6 @@
     cos, sin = jnp.cos(shift) * (1.0 / N), jnp.sin(shift) * (1.0 / N)
     value = jnp.where(part == n_part, cos, jnp.where(part == 0, sin, -sin))
     f_ref[0], f_ref[1] = halves(jnp.where(same, value, 0.0))
-
-
-def forward_kernel(
-    slot_ref, group_ref, plane_ref, count_ref, image_ref, coord_ref,
-    a_ref, idx_ref, pa_ref, pb_ref, wa_ref, wb_ref, live_ref, tw_ref, f_ref,
-    word_ref, v_ref, w_ref, zrow_ref, row_ref, local, send1, recv1, send2, recv2, sendz, recvz, sendi, recvi,
-):
-    slab, z, x, own = greet(True, True)
-
-    def word_copy(d):
-        peer = (z + d) % 8
-        return remote(word_ref, zrow_ref.at[z], sendz.at[d], recvz.at[z], (slab, peer, x))
-
-    def slab_copy(c, d):
-        peer = (slab + STEP8 * d) % 8
-        return remote(image_ref.at[:, :, peer, chunk(c)], v_ref.at[slab, :, :, chunk(c)], send1.at[c, d], recv1.at[c, slab], (peer, z, x))
-
-    def slab_wait(c, d):
-        peer = (slab + STEP8 * d) % 8
-        remote(image_ref.at[:, :, peer, chunk(c)], v_ref.at[peer, :, :, chunk(c)], send1.at[c, d], recv1.at[c, peer], (peer, z, x)).wait_recv()
-
-    def plane_copy(c, d):
-        peer = (own + STEP32 * d) % 32
-        return remote(w_ref.at[peer, :, chunk(c)], a_ref.at[own, :, chunk(c)], send2.at[c, d], recv2.at[c, own], place_of(peer, z))
-
-    def plane_wait(c, d):
-        peer = (own + STEP32 * d) % 32
-        remote(w_ref.at[peer, :, chunk(c)], a_ref.at[peer, :, chunk(c)], send2.at[c, d], recv2.at[c, peer], place_of(peer, z)).wait_recv()
-
-    def row_copy(d):
-        return remote(row_ref, idx_ref.at[own], sendi.at[d], recvi.at[own], place_of((own + d) % 32, z))
-
-    lane = lax.broadcasted_iota(jnp.int32, (1, 128), 1)
-    words = jnp.zeros((1, 128), jnp.int32)
-    for k in range(16):
-        tv = 32 * slab + group_ref[k]
-        word = slot_ref[k] + 256 * ((tv >> 2) & 7) + 2048 * tv
-        words = jnp.where(lane == 16 * z + k, word, words)
-    word_ref[...] = words
-    mine = pltpu.make_async_copy(image_ref.at[:, :, slab], v_ref.at[slab], local)
-    mine.start()
-    for c in range(CHUNKS):
-        each(8, lambda d: slab_copy(c, d).start())
-    each(8, lambda d: word_copy(d).start())
-    device_tables(slab, z, own, coord_ref, plane_ref, count_ref, pa_ref, pb_ref, wa_ref, wb_ref, live_ref, tw_ref, f_ref)
-
-    def word_wait(d):
-        peer = (z + d) % 8
-        remote(word_ref, zrow_ref.at[peer], sendz.at[d], recvz.at[peer], (slab, peer, x)).wait_recv()
-
-    each(8, word_wait)
-    zrow_ref[z] = word_ref[...]
-    row = zrow_ref[0]
-    for at in range(1, 8):
-        row = row + zrow_ref[at]
-    row_ref[...] = row
-    idx_ref[own] = row
-    mine.wait()
-    for c in range(CHUNKS):
-        each(8, lambda d: slab_wait(c, d))
-        if c == 0:
-            each(32, lambda d: row_copy(d).start())
-        butterfly(v_ref, w_ref, c)
-        each(32, lambda d: plane_copy(c, d).start())
-        a_ref[own, :, chunk(c)] = w_ref[own, :, chunk(c)]
-
-    def row_wait(d):
-        peer = (own + STEP32 * d) % 32
-        remote(row_ref, idx_ref.at[peer], sendi.at[d], recvi.at[peer], place_of(peer, z)).wait_recv()
-
-    each(32, row_wait)
-    for c in range(CHUNKS):
-        each(32, lambda d: plane_wait(c, d))
-    each(8, lambda d: word_copy(d).wait_send())
-    each(32, lambda d: row_copy(d).wait_send())
-    for c in range(CHUNKS):
-        each(8, lambda d: slab_copy(c, d).wait_send())
-        each(32, lambda d: plane_copy(c, d).wait_send())
 
 
 def backward_kernel(spot_ref, out_ref, w_ref, v_ref, local, keep, send1, recv1, send2, recv2):
@@ -375,20 +297,93 @@
     return jnp.where(at & 1 == 0, first, second)
 
 
-def gather_kernel(
-    idx_ref, a_ref, tw_ref, m_ref, m1_ref, w4_ref, f_ref, out_ref,
-    w_ref, full_ref, high_ref, low_ref, z_ref, s_ref, part_ref, right_ref, left_ref, sum_ref, sendr, recvr, sendl, recvl, sendp, recvp,
+def forward_kernel(
+    slot_ref, group_ref, plane_ref, count_ref, image_ref, coord_ref, obs_ref, m_ref, m1_ref, w4_ref, dr_ref, dl_ref,
+    vis_ref, g_ref, idx_ref, tw_ref, f_ref,
+    pa_ref, pb_ref, wa_ref, wb_ref, live_ref, tiles_ref, back_ref,
+    word_ref, v_ref, b_ref, zrow_ref, row_ref, a_ref, words_ref,
+    w_ref, full_ref, high_ref, low_ref, z_ref, s_ref, part_ref, right_ref, left_ref, sum_ref,
+    local, fetched, send1, recv1, send2, recv2, sendw, recvw, sendi, recvi, sendr, recvr, sendl, recvl, sendp, recvp,
+    sendq, recvq, sendt, recvt, sendu, recvu,
 ):
     slab, z, x, own = greet(True, True)
+
+    def word_copy(d):
+        peer = (z + d) % 8
+        return remote(word_ref, zrow_ref.at[z], sendw.at[d], recvw.at[z], (slab, peer, x))
+
+    def slab_copy(c, d):
+        peer = (slab + STEP8 * d) % 8
+        return remote(image_ref.at[:, :, peer, chunk(c)], v_ref.at[slab, :, :, chunk(c)], send1.at[c, d], recv1.at[c, slab], (peer, z, x))
+
+    def slab_wait(c, d):
+        peer = (slab + STEP8 * d) % 8
+        remote(image_ref.at[:, :, peer, chunk(c)], v_ref.at[peer, :, :, chunk(c)], send1.at[c, d], recv1.at[c, peer], (peer, z, x)).wait_recv()
+
+    def row_block_copy(c, d):
+        peer = (own + STEP32 * d) % 32
+        return remote(b_ref.at[peer, :, chunk(c)], a_ref.at[own, :, chunk(c)], send2.at[c, d], recv2.at[c, own], place_of(peer, z))
+
+    def row_block_wait(c, d):
+        peer = (own + STEP32 * d) % 32
+        remote(b_ref.at[peer, :, chunk(c)], a_ref.at[peer, :, chunk(c)], send2.at[c, d], recv2.at[c, peer], place_of(peer, z)).wait_recv()
+
+    def row_copy(d):
+        return remote(row_ref, idx_ref.at[own], sendi.at[d], recvi.at[own], place_of((own + d) % 32, z))
+
+    lane = lax.broadcasted_iota(jnp.int32, (1, 128), 1)
+    words = jnp.zeros((1, 128), jnp.int32)
+    for k in range(16):
+        tv = 32 * slab + group_ref[k]
+        word = slot_ref[k] + 256 * ((tv >> 2) & 7) + 2048 * tv
+        words = jnp.where(lane == 16 * z + k, word, words)
+    word_ref[...] = words
+    mine = pltpu.make_async_copy(image_ref.at[:, :, slab], v_ref.at[slab], local)
+    mine.start()
+    for c in range(CHUNKS):
+        each(8, lambda d: slab_copy(c, d).start())
+    each(8, lambda d: word_copy(d).start())
+    device_tables(slab, z, own, coord_ref, plane_ref, count_ref, pa_ref, pb_ref, wa_ref, wb_ref, live_ref, tw_ref, f_ref)
     spread_screens(w4_ref, w_ref)
     fill_columns(m1_ref, full_ref)
+
+    def word_wait(d):
+        peer = (z + d) % 8
+        remote(word_ref, zrow_ref.at[peer], sendw.at[d], recvw.at[peer], (slab, peer, x)).wait_recv()
+
+    each(8, word_wait)
+    zrow_ref[z] = word_ref[...]
+    row = zrow_ref[0]
+    for at in range(1, 8):
+        row = row + zrow_ref[at]
+    row_ref[...] = row
+    idx_ref[own] = row
+    mine.wait()
+    for c in range(CHUNKS):
+        each(8, lambda d: slab_wait(c, d))
+        if c == 0:
+            each(32, lambda d: row_copy(d).start())
+        butterfly(v_ref, b_ref, c)
+        each(32, lambda d: row_block_copy(c, d).start())
+        a_ref[own, :, chunk(c)] = b_ref[own, :, chunk(c)]
+
+    def row_wait(d):
+        peer = (own + STEP32 * d) % 32
+        remote(row_ref, idx_ref.at[peer], sendi.at[d], recvi.at[peer], place_of(peer, z)).wait_recv()
+
+    each(32, row_wait)
+    fetch = pltpu.make_async_copy(idx_ref, words_ref, fetched)
+    fetch.start()
+    for c in range(CHUNKS):
+        each(32, lambda d: row_block_wait(c, d))
+
     cos, sin = (m_ref[0], m_ref[1]), (m_ref[2], m_ref[3])
     twr = jnp.concatenate([tw_ref[0]] * 2, axis=1)
     twi = jnp.concatenate([tw_ref[1]] * 2, axis=1)
     total = [None] * 4
     for xx in range(4):
-        ar = a_ref[:, xx, 0].reshape(256, 256)
-        ai = a_ref[:, xx, 1].reshape(256, 256)
+        ar = jnp.concatenate([a_ref[4 * a1 + xx, 0] for a1 in range(8)], axis=0)
+        ai = jnp.concatenate([a_ref[4 * a1 + xx, 1] for a1 in range(8)], axis=0)
         br, bi = halves(ar * twr - ai * twi), halves(ar * twi + ai * twr)
         ur = dot3(cos, br) + dot3(sin, bi)
         ui = dot3(cos, bi) - dot3(sin, br)
@@ -422,7 +417,7 @@
                 for half in range(2):
                     res, ims = [], []
                     for k in range(8):
-                        word = idx_ref[d, 0, zc * 16 + half * 8 + k]
+                        word = words_ref[d, 0, zc * 16 + half * 8 + k]
                         spot, tv = word & 2047, word >> 11
                         zr, zi = z_ref[0, spot], z_ref[1, spot]
                         wr, wi = w_ref[tv, 0], w_ref[tv, 1]
@@ -474,6 +469,7 @@
 
         return carry
 
+    fetch.wait()
     lax.fori_loop(0, 8, outward, 0)
     for u in range(2):
         left_copy(2, u).wait_recv()
@@ -486,14 +482,14 @@
 
     def plane_copy(d):
         peer = (own + STEP32 * d) % 32
-        return remote(sum_ref.at[block(peer)], out_ref.at[block(own)], sendp.at[d], recvp.at[own], place_of(peer, z))
+        return remote(sum_ref.at[block(peer)], tiles_ref.at[block(own)], sendp.at[d], recvp.at[own], place_of(peer, z))
 
     def plane_wait(d):
         peer = (own + STEP32 * d) % 32
-        remote(sum_ref.at[block(peer)], out_ref.at[block(peer)], sendp.at[d], recvp.at[peer], place_of(peer, z)).wait_recv()
+        remote(sum_ref.at[block(peer)], tiles_ref.at[block(peer)], sendp.at[d], recvp.at[peer], place_of(peer, z)).wait_recv()
 
     each(32, lambda d: plane_copy(d).start())
-    out_ref[block(own), :] = sum_ref[block(own), :]
+    tiles_ref[block(own), :] = sum_ref[block(own), :]
     each(32, plane_wait)
     for u in range(2):
         for h in range(4):
@@ -501,88 +497,20 @@
             if h < 3:
                 left_copy(h, u).wait_send()
     each(32, lambda d: plane_copy(d).wait_send())
-
-
-def scatter_kernel(idx_ref, c_ref, tw_ref, m_ref, m1_ref, w4_ref, f_ref, out_ref, w_ref, full_ref, l_ref, crep_ref, z0_ref, z1_ref):
-    spread_screens(w4_ref, w_ref)
-    fill_columns(m1_ref, full_ref)
-    spread = dot3(halves(c_ref[...]), (f_ref[0], f_ref[1]))
-    for at in range(4):
-        crep_ref[at] = spread[:, 128 * at : 128 * at + 128]
-
-    def clear(step, carry):
-        spots = pl.ds(pl.multiple_of(step * 128, 128), 128)
-        zero = jnp.zeros((2, 128, 8, 128), F32)
-        z0_ref[:, spots] = zero
-        z1_ref[:, spots] = zero
-        return carry
-
-    lax.fori_loop(0, 16, clear, 0)
-
-    def add(it, carry):
-        for k in range(16):
-            z_ref = (z0_ref, z1_ref)[k % 2]
-            half, row = k // 8, k % 8
-            word = idx_ref[it % 32, 0, it // 32 * 16 + k]
-            spot, tv = word & 2047, word >> 11
-            cr = jnp.broadcast_to(crep_ref[2 * half, pl.ds(it * 8 + row, 1), :], (8, 128))
-            ci = jnp.broadcast_to(crep_ref[2 * half + 1, pl.ds(it * 8 + row, 1), :], (8, 128))
-            wr, wi = w_ref[tv, 0], w_ref[tv, 1]
-            z_ref[0, spot] += cr * wr + ci * wi
-            z_ref[1, spot] += ci * wr - cr * wi
-        return carry
-
-    lax.fori_loop(0, 256, add, 0)
-
-    def stage(step, carry):
-        res = None
-        for block in range(8):
-            lanes = slice(256 * block, 256 * block + 256)
-            spots = [pl.ds(pl.multiple_of(t % 8 * 256 + step * 32, 32), 32) for t in (2 * block, 2 * block + 1)]
-            parts = [(z0_ref[block // 4, at] + z1_ref[block // 4, at]).reshape(256, 128) for at in spots]
-            left = halves(jnp.concatenate(parts, axis=1))
-            part = dot3(left, (full_ref[0, :, lanes], full_ref[1, :, lanes]), dot_t)
-            res = part if res is None else res + part
-        rows = pl.ds(pl.multiple_of(step * 256, 256), 256)
-        l_ref[0, rows, :], l_ref[1, rows, :] = res[:, 0:128], res[:, 128:256]
-        return carry
-
-    lax.fori_loop(0, 8, stage, 0)
-
-    wide = []
-    for at in range(2):
-        wide += halves(jnp.concatenate([l_ref[at, pl.ds(b, 256, stride=8), :] for b in range(8)], axis=1))
-    cos, sin = (m_ref[0], m_ref[1]), (m_ref[2], m_ref[3])
-    twr = jnp.concatenate([tw_ref[0]] * 2, axis=1)
-    twi = jnp.concatenate([tw_ref[1]] * 2, axis=1)
-    for x in range(4):
-        place = placing(x)
-        pieces = [dot_t(piece, place).astype(BF16) for piece in wide]
-        ur, ui = (pieces[0], pieces[1]), (pieces[2], pieces[3])
-        ar = dot3(cos, ur) - dot3(sin, ui)
-        ai = dot3(cos, ui) + dot3(sin, ur)
-        out_ref[:, x, 0] = (ar * twr + ai * twi).reshape(8, 32, 256)
-        out_ref[:, x, 1] = (ai * twr - ar * twi).reshape(8, 32, 256)
-
-
-def hdot(left, right):
-    return jnp.dot(left, right, preferred_element_type=F32, precision=HIGHEST)
-
-
-def hdot_t(left, right):
-    return lax.dot_general(left, right, (((1,), (1,)), ((), ())), preferred_element_type=F32, precision=HIGHEST)
-
-
-def subgrid_kernel(t_ref, right_ref, left_ref, wa_ref, wb_ref, pa_ref, pb_ref, obs_ref, live_ref, vis_ref, g_ref, out_ref, send1, recv1, sendr, recvr, sendl, recvl):
-    slab, z, x, own = greet(True, True)
-    tiles = jnp.concatenate([t_ref[pl.ds(k, 32, stride=8), :] for k in range(8)], axis=0)
-    both = hdot(tiles, right_ref[...])
+    each(8, lambda d: word_copy(d).wait_send())
+    each(32, lambda d: row_copy(d).wait_send())
+    for c in range(CHUNKS):
+        each(8, lambda d: slab_copy(c, d).wait_send())
+        each(32, lambda d: row_block_copy(c, d).wait_send())
+
+    tiles = jnp.concatenate([tiles_ref[pl.ds(k, 32, stride=8), :] for k in range(8)], axis=0)
+    both = hdot(tiles, dr_ref[...])
     rows = []
     for k in range(8):
         cut = slice(32 * k, 32 * k + 32)
         y, iy = both[cut, 0:128], both[cut, 128:256]
         column = jnp.concatenate([jnp.concatenate([y, iy], axis=1), jnp.concatenate([iy, -y], axis=1)], axis=0)
-        s_both = hdot(left_ref[0], column)
+        s_both = hdot(dl_ref[0], column)
         s, i_s = s_both[:, 0:128], s_both[:, 128:256]
         wa, wb = wa_ref[k], wb_ref[k]
         weighted = wa * s + wb * i_s
@@ -606,41 +534,41 @@
             i_found.append(back[32:64])
         c, ic = jnp.concatenate(found, axis=1), jnp.concatenate(i_found, axis=1)
         r, ir = wa * c - wb * ic, wa * ic + wb * c
-        rows.append(hdot(left_ref[1], jnp.concatenate([r, ir], axis=0)))
-    tile = hdot_t(jnp.concatenate(rows, axis=0), right_ref[:, 0:128])
+        rows.append(hdot(dl_ref[1], jnp.concatenate([r, ir], axis=0)))
+    tile = hdot_t(jnp.concatenate(rows, axis=0), dr_ref[:, 0:128])
     for k in range(8):
-        out_ref[pl.ds(k, 32, stride=8), :] = tile[32 * k : 32 * k + 32]
+        back_ref[pl.ds(k, 32, stride=8), :] = tile[32 * k : 32 * k + 32]
 
     def block(d):
         return pl.ds(pl.multiple_of(8 * d, 8), 8)
 
     def plane_copy(d):
         peer = (own + STEP32 * d) % 32
-        return remote(out_ref.at[block(peer)], g_ref.at[z, block(own)], send1.at[d], recv1.at[own], place_of(peer, z))
+        return remote(back_ref.at[block(peer)], g_ref.at[z, block(own)], sendq.at[d], recvq.at[own], place_of(peer, z))
 
     def plane_wait(d):
         peer = (own + STEP32 * d) % 32
-        remote(out_ref.at[block(peer)], g_ref.at[z, block(peer)], send1.at[d], recv1.at[peer], place_of(peer, z)).wait_recv()
+        remote(back_ref.at[block(peer)], g_ref.at[z, block(peer)], sendq.at[d], recvq.at[peer], place_of(peer, z)).wait_recv()
 
     each(32, lambda d: plane_copy(d).start())
-    g_ref[z, block(own), :] = out_ref[block(own), :]
+    g_ref[z, block(own), :] = back_ref[block(own), :]
     each(32, plane_wait)
 
     def right_copy(h, u):
         ref = g_ref.at[(z + 8 - h) % 8, pl.ds(64 * u, 64)]
-        return remote(ref, ref, sendr.at[h, u], recvr.at[h, u], (slab, (z + 1) % 8, x))
+        return remote(ref, ref, sendt.at[h, u], recvt.at[h, u], (slab, (z + 1) % 8, x))
 
     def left_copy(h, u):
         ref = g_ref.at[(z + h) % 8, pl.ds(64 * u, 64)]
-        return remote(ref, ref, sendl.at[h, u], recvl.at[h, u], (slab, (z + 7) % 8, x))
+        return remote(ref, ref, sendu.at[h, u], recvu.at[h, u], (slab, (z + 7) % 8, x))
 
     def right_wait(h, u):
         ref = g_ref.at[(z + 7 - h) % 8, pl.ds(64 * u, 64)]
-        remote(ref, ref, sendr.at[h, u], recvr.at[h, u], (slab, (z + 1) % 8, x)).wait_recv()
+        remote(ref, ref, sendt.at[h, u], recvt.at[h, u], (slab, (z + 1) % 8, x)).wait_recv()
 
     def left_wait(h, u):
         ref = g_ref.at[(z + 1 + h) % 8, pl.ds(64 * u, 64)]
-        remote(ref, ref, sendl.at[h, u], recvl.at[h, u], (slab, (z + 7) % 8, x)).wait_recv()
+        remote(ref, ref, sendu.at[h, u], recvu.at[h, u], (slab, (z + 7) % 8, x)).wait_recv()
 
     for h in range(4):
         for u in range(4):
@@ -662,6 +590,76 @@
                 left_copy(h, u).wait_send()
 
 
+def scatter_kernel(idx_ref, c_ref, tw_ref, m_ref, m1_ref, w4_ref, f_ref, out_ref, w_ref, full_ref, l_ref, crep_ref, z0_ref, z1_ref):
+    spread_screens(w4_ref, w_ref)
+    fill_columns(m1_ref, full_ref)
+    spread = dot3(halves(c_ref[...]), (f_ref[0], f_ref[1]))
+    for at in range(4):
+        crep_ref[at] = spread[:, 128 * at : 128 * at + 128]
+
+    def clear(step, carry):
+        spots = pl.ds(pl.multiple_of(step * 128, 128), 128)
+        zero = jnp.zeros((2, 128, 8, 128), F32)
+        z0_ref[:, spots] = zero
+        z1_ref[:, spots] = zero
+        return carry
+
+    lax.fori_loop(0, 16, clear, 0)
+
+    def add(it, carry):
+        for k in range(16):
+            z_ref = (z0_ref, z1_ref)[k % 2]
+            half, row = k // 8, k % 8
+            word = idx_ref[it % 32, 0, it // 32 * 16 + k]
+            spot, tv = word & 2047, word >> 11
+            cr = jnp.broadcast_to(crep_ref[2 * half, pl.ds(it * 8 + row, 1), :], (8, 128))
+            ci = jnp.broadcast_to(crep_ref[2 * half + 1, pl.ds(it * 8 + row, 1), :], (8, 128))
+            wr, wi = w_ref[tv, 0], w_ref[tv, 1]
+            z_ref[0, spot] += cr * wr + ci * wi
+            z_ref[1, spot] += ci * wr - cr * wi
+        return carry
+
+    lax.fori_loop(0, 256, add, 0)
+
+    def stage(step, carry):
+        res = None
+        for block in range(8):
+            lanes = slice(256 * block, 256 * block + 256)
+            spots = [pl.ds(pl.multiple_of(t % 8 * 256 + step * 32, 32), 32) for t in (2 * block, 2 * block + 1)]
+            parts = [(z0_ref[block // 4, at] + z1_ref[block // 4, at]).reshape(256, 128) for at in spots]
+            left = halves(jnp.concatenate(parts, axis=1))
+            part = dot3(left, (full_ref[0, :, lanes], full_ref[1, :, lanes]), dot_t)
+            res = part if res is None else res + part
+        rows = pl.ds(pl.multiple_of(step * 256, 256), 256)
+        l_ref[0, rows, :], l_ref[1, rows, :] = res[:, 0:128], res[:, 128:256]
+        return carry
+
+    lax.fori_loop(0, 8, stage, 0)
+
+    wide = []
+    for at in range(2):
+        wide += halves(jnp.concatenate([l_ref[at, pl.ds(b, 256, stride=8), :] for b in range(8)], axis=1))
+    cos, sin = (m_ref[0], m_ref[1]), (m_ref[2], m_ref[3])
+    twr = jnp.concatenate([tw_ref[0]] * 2, axis=1)
+    twi = jnp.concatenate([tw_ref[1]] * 2, axis=1)
+    for x in range(4):
+        place = placing(x)
+        pieces = [dot_t(piece, place).astype(BF16) for piece in wide]
+        ur, ui = (pieces[0], pieces[1]), (pieces[2], pieces[3])
+        ar = dot3(cos, ur) - dot3(sin, ui)
+        ai = dot3(cos, ui) + dot3(sin, ur)
+        out_ref[:, x, 0] = (ar * twr + ai * twi).reshape(8, 32, 256)
+        out_ref[:, x, 1] = (ai * twr - ar * twi).reshape(8, 32, 256)
+
+
+def hdot(left, right):
+    return jnp.dot(left, right, preferred_element_type=F32, precision=HIGHEST)
+
+
+def hdot_t(left, right):
+    return lax.dot_general(left, right, (((1,), (1,)), ((), ())), preferred_element_type=F32, precision=HIGHEST)
+
+
 def subgrid_tables():
     index = np.arange(SUB)
     cos, sin = unit(index[:, None] * (index[None, :] - SUB // 2), SUB)
@@ -701,44 +699,31 @@
     rows, columns, screens = row_tables(), column_tables(), screen_tables()
     right, left = subgrid_tables()
 
-    a, words, pa, pb, wa, wb, live, tw, spread = call(
+    vis, every, words, tw, spread = call(
         forward_kernel,
         (
-            f32(32, 2, 32, 256),
+            f32(32, 128),
+            f32(8, 256, 128),
             jax.ShapeDtypeStruct((32, 1, 128), jnp.int32),
-            f32(2, 16, 32, 128),
-            f32(2, 16, 32, 128),
-            f32(8, 32, 128),
-            f32(8, 32, 128),
-            f32(16, 128),
             f32(2, 256, 128),
             jax.ShapeDtypeStruct((2, 128, 512), BF16),
         ),
-        [SMEM] * 4 + [ANY] + in_vmem(1),
+        [SMEM] * 4 + [ANY] + in_vmem(7),
         [
+            pltpu.VMEM((2, 16, 32, 128), F32),
+            pltpu.VMEM((2, 16, 32, 128), F32),
+            pltpu.VMEM((8, 32, 128), F32),
+            pltpu.VMEM((8, 32, 128), F32),
+            pltpu.VMEM((16, 128), F32),
+            pltpu.VMEM((256, 128), F32),
+            pltpu.VMEM((256, 128), F32),
             pltpu.VMEM((1, 128), jnp.int32),
             pltpu.VMEM((8, 2, 4, 32, 256), F32),
             pltpu.VMEM((32, 2, 32, 256), F32),
             pltpu.VMEM((8, 1, 128), jnp.int32),
             pltpu.VMEM((1, 128), jnp.int32),
-            DMA,
-            DMA((CHUNKS, 8)),
-            DMA((CHUNKS, 8)),
-            DMA((CHUNKS, 32)),
-            DMA((CHUNKS, 32)),
-            DMA((8,)),
-            DMA((8,)),
-            DMA((32,)),
-            DMA((32,)),
-        ],
-        collective_id=0,
-    )(tile_slot, tile_group[:, 0], w_plane, vis_count, model_image.reshape(2, 4, 8, 32, 256), vis_coords.reshape(32, 128))
-    a = a.reshape(8, 4, 2, 32, 256)
-    tiles = call(
-        gather_kernel,
-        f32(256, 128),
-        [SMEM] + in_vmem(6),
-        [
+            pltpu.VMEM((32, 2, 32, 256), F32),
+            pltpu.SMEM((32, 1, 128), jnp.int32),
             pltpu.VMEM((256, 2, 8, 128), F32),
             pltpu.VMEM((2, 256, 2048), BF16),
             pltpu.VMEM((2, 2048, 128), F32),
@@ -749,23 +734,33 @@
             pltpu.VMEM((4, 256, 128), F32),
             pltpu.VMEM((3, 256, 128), F32),
             pltpu.VMEM((256, 128), F32),
+            DMA,
+            DMA,
+            DMA((CHUNKS, 8)),
+            DMA((CHUNKS, 8)),
+            DMA((CHUNKS, 32)),
+            DMA((CHUNKS, 32)),
+            DMA((8,)),
+            DMA((8,)),
+            DMA((32,)),
+            DMA((32,)),
             DMA((4, 2)),
             DMA((4, 2)),
             DMA((3, 2)),
             DMA((3, 2)),
             DMA((32,)),
             DMA((32,)),
+            DMA((32,)),
+            DMA((32,)),
+            DMA((4, 4)),
+            DMA((4, 4)),
+            DMA((3, 4)),
+            DMA((3, 4)),
         ],
-        collective_id=3,
-    )(words, a, tw, rows, columns, screens, spread)
-    vis, every = call(
-        subgrid_kernel,
-        (f32(32, 128), f32(8, 256, 128)),
-        in_vmem(9),
-        [pltpu.VMEM((256, 128), F32), DMA((32,)), DMA((32,)), DMA((4, 4)), DMA((4, 4)), DMA((3, 4)), DMA((3, 4))],
-        collective_id=1,
+        collective_id=0,
     )(
-        tiles, right, left, wa, wb, pa, pb, vis_observed.reshape(32, 128), live
+        tile_slot, tile_group[:, 0], w_plane, vis_count, model_image.reshape(2, 4, 8, 32, 256),
+        vis_coords.reshape(32, 128), vis_observed.reshape(32, 128), rows, columns, screens, right, left,
     )
     every = every.reshape(2048, 128)
     spots = call(

time: 249 us -> 236 us (0.948)
  Pallas kernels: 245 us -> 231 us
    pallas_call x3 -> x1, Pallas kernels: 152 us -> 138 us  [per_device(): call(forward_kernel, (f32(32, 128), f32(8, 256, 128), jax.ShapeDtypeStruc...]
where the time goes in v4:
time: 236 us
  Pallas kernels  231 us (98%)
  local copies, waits for them, and re-layouts  3.66 us (2%)
    pallas_call x1, Pallas kernels, per_device(): call(forward_kernel, (f32(32, 128), f32(8, 256, 128), jax.ShapeDtypeStruc...  138 us
    pallas_call x1, Pallas kernels, per_device(): call(backward_kernel, f32(8, 2, 4, 32, 256), [ANY], [pltpu.VMEM((32, 2, 3...  55.5 us
    pallas_call x1, Pallas kernels, per_device(): call(scatter_kernel, f32(8, 4, 2, 32, 256), [SMEM] + in_vmem(6), [pltpu.V...  38.1 us

profile of v4, /device:TPU:1, one launch (start us, length us, event | category | flops | bytes accessed | tf_op | source)
XLA Modules:
  0.0 235.7 jit_solution(1784168900007975163)
XLA Ops:
  0.6 137.7 %shard_map.131 = (f32[32,128]{1,0:T(8,128)}, f32[8,256,128]{2,1,0:T(8,128)}, s32[32,1,128]{2,1,0:T(1,128)}, f32[2,256,128]{2,1,0:T(8,128)}, bf16[2,128,512]{2,1,0:T(8,128)(2,1)}) custom-call(s32[16]{0:T(128)} %slot_ref.1, s32[16]{0:T(128)} %bitcast.17, s32[16]{0:T(128)} %plane_ref.1, s32[16]{0:T(128)} %count_ref.1, f32[2,4,8,32,256]{4,3,2,1,0:T(8,128)} %bitcast.11, ...), custom_call_target="tpu_custom_call" | custom-call | tf_op jit(solution)/shard_map/pallas_call | solution.py:702
  138.4 38.1 %shard_map.132 = f32[8,4,2,32,256]{4,3,2,1,0:T(8,128)} custom-call(s32[32,1,128]{2,1,0:T(1,128)} %get-tuple-element.7.idx_ref, f32[2048,128]{1,0:T(8,128)} %bitcast.13, f32[2,256,128]{2,1,0:T(8,128)} %get-tuple-element.9.tw_ref, bf16[4,256,256]{2,1,0:T(8,128)(2,1)} %constant.10.clone.m_ref, bf16[4,128,1024]{2,1,0:T(8,128)(2,1)} %constant.11.clone.m1_ref, ...), custom_call_target="tpu_custom_call" | custom-call | tf_op jit(solution)/shard_map/pallas_call | solution.py:766
  176.5 0.0 copy-start
  176.5 1.6 copy-done
  178.1 55.5 %shard_map.133 = f32[8,2,4,32,256]{4,3,2,1,0:T(8,128)S(1)} custom-call(f32[32,2,32,256]{3,2,1,0:T(8,128)S(1)} %bitcast.10), custom_call_target="tpu_custom_call" | custom-call | tf_op jit(solution)/shard_map/pallas_call | solution.py:779
  233.6 0.0 copy-start.1
  233.6 1.5 copy.14
  235.1 0.0 copy-done.1
  235.1 0.6 copy.16
Async XLA Ops:
  176.5 1.6 copy-start
  233.6 1.5 copy-start.1

commit v5 on v4

--- a/solution.py
+++ b/solution.py
@@ -21,6 +21,7 @@
 HIGHEST = lax.Precision.HIGHEST
 MESH = pl.DeviceIdType.MESH
 ANY = pl.BlockSpec(memory_space=pl.ANY)
+HBM = pl.BlockSpec(memory_space=pltpu.HBM)
 DMA = pltpu.SemaphoreType.DMA
 
 
@@ -275,12 +276,13 @@
 
 
 def fill_columns(m1_ref, full_ref):
-    for h in range(2):
+    for at, h in enumerate((0, 1, 0)):
         cos, sin = m1_ref[h], m1_ref[2 + h]
-        full_ref[h, 0:128, 0:1024] = cos
-        full_ref[h, 0:128, 1024:2048] = -sin
-        full_ref[h, 128:256, 0:1024] = sin
-        full_ref[h, 128:256, 1024:2048] = cos
+        top, mid, end = 256 * at, 256 * at + 128, 256 * at + 256
+        full_ref[top:mid, 0:1024] = cos
+        full_ref[top:mid, 1024:2048] = -sin
+        full_ref[mid:end, 0:1024] = sin
+        full_ref[mid:end, 1024:2048] = cos
 
 
 def row_sums(values):
@@ -298,13 +300,13 @@
 
 
 def forward_kernel(
-    slot_ref, group_ref, plane_ref, count_ref, image_ref, coord_ref, obs_ref, m_ref, m1_ref, w4_ref, dr_ref, dl_ref,
-    vis_ref, g_ref, idx_ref, tw_ref, f_ref,
+    slot_ref, group_ref, plane_ref, count_ref, image_ref, coord_ref, obs_ref, dr_ref, dl_ref, m_any, m1_any, w4_any,
+    vis_ref, g_ref, idx_ref, rows_ref, tw_ref, f_ref,
     pa_ref, pb_ref, wa_ref, wb_ref, live_ref, tiles_ref, back_ref,
     word_ref, v_ref, b_ref, zrow_ref, row_ref, a_ref, words_ref,
     w_ref, full_ref, high_ref, low_ref, z_ref, s_ref, part_ref, right_ref, left_ref, sum_ref,
     local, fetched, send1, recv1, send2, recv2, sendw, recvw, sendi, recvi, sendr, recvr, sendl, recvl, sendp, recvp,
-    sendq, recvq, sendt, recvt, sendu, recvu,
+    sendq, recvq, sendt, recvt, sendu, recvu, m_ref, m1_ref, w4_ref, table,
 ):
     slab, z, x, own = greet(True, True)
 
@@ -343,7 +345,15 @@
     for c in range(CHUNKS):
         each(8, lambda d: slab_copy(c, d).start())
     each(8, lambda d: word_copy(d).start())
+    tables = [
+        pltpu.make_async_copy(src, dst, table.at[at])
+        for at, (src, dst) in enumerate(((m_any, m_ref), (m1_any, m1_ref), (w4_any, w4_ref)))
+    ]
+    for copy in tables:
+        copy.start()
     device_tables(slab, z, own, coord_ref, plane_ref, count_ref, pa_ref, pb_ref, wa_ref, wb_ref, live_ref, tw_ref, f_ref)
+    for copy in tables:
+        copy.wait()
     spread_screens(w4_ref, w_ref)
     fill_columns(m1_ref, full_ref)
 
@@ -374,6 +384,7 @@
     each(32, row_wait)
     fetch = pltpu.make_async_copy(idx_ref, words_ref, fetched)
     fetch.start()
+    rows_ref[...] = 8 * (idx_ref[...] & 2047) + 262144 * (idx_ref[...] >> 11)
     for c in range(CHUNKS):
         each(32, lambda d: row_block_wait(c, d))
 
@@ -403,8 +414,7 @@
         rows = pl.ds(pl.multiple_of(part * 512, 512), 512)
         lanes = pl.ds(pl.multiple_of(block * 256, 256), 256)
         left = tuple(jnp.concatenate([ref[0, rows, :], ref[1, rows, :]], axis=1).astype(BF16) for ref in (high_ref, low_ref))
-        right = (full_ref[0, :, lanes], full_ref[1, :, lanes])
-        res = dot3(left, right)
+        res = dot(jnp.concatenate([left[0], left[0], left[1]], axis=1), full_ref[:, lanes])
         z_ref[block // 4, pl.ds(pl.multiple_of(block % 4 * 512 + part * 64, 64), 64)] = res[:, 0:128].reshape(64, 8, 128)
         z_ref[block // 4, pl.ds(pl.multiple_of(block % 4 * 512 + 256 + part * 64, 64), 64)] = res[:, 128:256].reshape(64, 8, 128)
         return carry
@@ -552,7 +562,19 @@
 
     each(32, lambda d: plane_copy(d).start())
     g_ref[z, block(own), :] = back_ref[block(own), :]
-    each(32, plane_wait)
+
+    def quarter_wait(u):
+        def one(step, carry):
+            peer = 8 * u + step
+
+            @pl.when(peer != own)
+            def _():
+                ref = g_ref.at[z, block(peer)]
+                remote(ref, ref, sendq.at[0], recvq.at[peer], place_of((own + 1) % 32, z)).wait_recv()
+
+            return carry
+
+        lax.fori_loop(0, 8, one, 0)
 
     def right_copy(h, u):
         ref = g_ref.at[(z + 8 - h) % 8, pl.ds(64 * u, 64)]
@@ -574,6 +596,8 @@
         for u in range(4):
             if h:
                 right_wait(h - 1, u)
+            else:
+                quarter_wait(u)
             right_copy(h, u).start()
             if h < 3:
                 if h:
@@ -590,33 +614,47 @@
                 left_copy(h, u).wait_send()
 
 
-def scatter_kernel(idx_ref, c_ref, tw_ref, m_ref, m1_ref, w4_ref, f_ref, out_ref, w_ref, full_ref, l_ref, crep_ref, z0_ref, z1_ref):
+def scatter_kernel(
+    idx_ref, tw_ref, f_ref, c_any, m_any, m1_any, w4_any, out_ref,
+    w_ref, full_ref, l_ref, crep_ref, z0_ref, z1_ref, c_ref, m_ref, m1_ref, w4_ref, table,
+):
+    tables = [
+        pltpu.make_async_copy(src, dst, table.at[at])
+        for at, (src, dst) in enumerate(((w4_any, w4_ref), (m1_any, m1_ref), (c_any, c_ref), (m_any, m_ref)))
+    ]
+    for copy in tables:
+        copy.start()
+
+    def clear(step, carry):
+        spots = pl.ds(pl.multiple_of(step * 128, 128), 128)
+        zero = jnp.zeros((2, 128, 8, 128), F32)
+        z0_ref[:, spots] = zero
+        z1_ref[:, spots] = zero
+        return carry
+
+    lax.fori_loop(0, 16, clear, 0)
+    for copy in tables:
+        copy.wait()
     spread_screens(w4_ref, w_ref)
     fill_columns(m1_ref, full_ref)
     spread = dot3(halves(c_ref[...]), (f_ref[0], f_ref[1]))
     for at in range(4):
         crep_ref[at] = spread[:, 128 * at : 128 * at + 128]
 
-    def clear(step, carry):
-        spots = pl.ds(pl.multiple_of(step * 128, 128), 128)
-        zero = jnp.zeros((2, 128, 8, 128), F32)
-        z0_ref[:, spots] = zero
-        z1_ref[:, spots] = zero
-        return carry
-
-    lax.fori_loop(0, 16, clear, 0)
+    w_rows = w_ref.reshape(4096, 128)
+    sets = (z0_ref.reshape(32768, 128), z1_ref.reshape(32768, 128))
 
     def add(it, carry):
         for k in range(16):
-            z_ref = (z0_ref, z1_ref)[k % 2]
+            z_rows = sets[k % 2]
             half, row = k // 8, k % 8
             word = idx_ref[it % 32, 0, it // 32 * 16 + k]
-            spot, tv = word & 2047, word >> 11
+            spot, turn_row = pl.multiple_of(word & 16383, 8), pl.multiple_of(word >> 14, 8)
             cr = jnp.broadcast_to(crep_ref[2 * half, pl.ds(it * 8 + row, 1), :], (8, 128))
             ci = jnp.broadcast_to(crep_ref[2 * half + 1, pl.ds(it * 8 + row, 1), :], (8, 128))
-            wr, wi = w_ref[tv, 0], w_ref[tv, 1]
-            z_ref[0, spot] += cr * wr + ci * wi
-            z_ref[1, spot] += ci * wr - cr * wi
+            wr, wi = w_rows[pl.ds(turn_row, 8), :], w_rows[pl.ds(turn_row + 8, 8), :]
+            z_rows[pl.ds(spot, 8), :] += cr * wr + ci * wi
+            z_rows[pl.ds(spot + 16384, 8), :] += ci * wr - cr * wi
         return carry
 
     lax.fori_loop(0, 256, add, 0)
@@ -628,7 +666,7 @@
             spots = [pl.ds(pl.multiple_of(t % 8 * 256 + step * 32, 32), 32) for t in (2 * block, 2 * block + 1)]
             parts = [(z0_ref[block // 4, at] + z1_ref[block // 4, at]).reshape(256, 128) for at in spots]
             left = halves(jnp.concatenate(parts, axis=1))
-            part = dot3(left, (full_ref[0, :, lanes], full_ref[1, :, lanes]), dot_t)
+            part = dot3(left, (full_ref[0:256, lanes], full_ref[256:512, lanes]), dot_t)
             res = part if res is None else res + part
         rows = pl.ds(pl.multiple_of(step * 256, 256), 256)
         l_ref[0, rows, :], l_ref[1, rows, :] = res[:, 0:128], res[:, 128:256]
@@ -699,16 +737,17 @@
     rows, columns, screens = row_tables(), column_tables(), screen_tables()
     right, left = subgrid_tables()
 
-    vis, every, words, tw, spread = call(
+    vis, every, _, words, tw, spread = call(
         forward_kernel,
         (
             f32(32, 128),
             f32(8, 256, 128),
             jax.ShapeDtypeStruct((32, 1, 128), jnp.int32),
+            jax.ShapeDtypeStruct((32, 1, 128), jnp.int32),
             f32(2, 256, 128),
             jax.ShapeDtypeStruct((2, 128, 512), BF16),
         ),
-        [SMEM] * 4 + [ANY] + in_vmem(7),
+        [SMEM] * 4 + [ANY] + in_vmem(4) + [ANY] * 3,
         [
             pltpu.VMEM((2, 16, 32, 128), F32),
             pltpu.VMEM((2, 16, 32, 128), F32),
@@ -725,7 +764,7 @@
             pltpu.VMEM((32, 2, 32, 256), F32),
             pltpu.SMEM((32, 1, 128), jnp.int32),
             pltpu.VMEM((256, 2, 8, 128), F32),
-            pltpu.VMEM((2, 256, 2048), BF16),
+            pltpu.VMEM((768, 2048), BF16),
             pltpu.VMEM((2, 2048, 128), F32),
             pltpu.VMEM((2, 2048, 128), F32),
             pltpu.VMEM((2, 2048, 8, 128), F32),
@@ -756,30 +795,39 @@
             DMA((4, 4)),
             DMA((3, 4)),
             DMA((3, 4)),
+            pltpu.VMEM((4, 256, 256), BF16),
+            pltpu.VMEM((4, 128, 1024), BF16),
+            pltpu.VMEM((64, 2, 8, 128), F32),
+            DMA((3,)),
         ],
         collective_id=0,
     )(
         tile_slot, tile_group[:, 0], w_plane, vis_count, model_image.reshape(2, 4, 8, 32, 256),
-        vis_coords.reshape(32, 128), vis_observed.reshape(32, 128), rows, columns, screens, right, left,
+        vis_coords.reshape(32, 128), vis_observed.reshape(32, 128), right, left, rows, columns, screens,
     )
     every = every.reshape(2048, 128)
     spots = call(
         scatter_kernel,
         f32(8, 4, 2, 32, 256),
-        [SMEM] + in_vmem(6),
+        [SMEM] + in_vmem(2) + [ANY] * 4,
         [
             pltpu.VMEM((256, 2, 8, 128), F32),
-            pltpu.VMEM((2, 256, 2048), BF16),
+            pltpu.VMEM((768, 2048), BF16),
             pltpu.VMEM((2, 2048, 128), F32),
             pltpu.VMEM((4, 2048, 128), F32),
             pltpu.VMEM((2, 2048, 8, 128), F32),
             pltpu.VMEM((2, 2048, 8, 128), F32),
+            pltpu.VMEM((2048, 128), F32),
+            pltpu.VMEM((4, 256, 256), BF16),
+            pltpu.VMEM((4, 128, 1024), BF16),
+            pltpu.VMEM((64, 2, 8, 128), F32),
+            DMA((4,)),
         ],
-    )(words, every, tw, rows, columns, screens, spread)
+    )(words, tw, spread, every, rows, columns, screens)
     image = call(
         backward_kernel,
         f32(8, 2, 4, 32, 256),
-        [ANY],
+        [HBM],
         [
             pltpu.VMEM((32, 2, 32, 256), F32),
             pltpu.VMEM((8, 2, 4, 32, 256), F32),

time: 236 us -> 232 us (0.983)
  Pallas kernels: 231 us -> 227 us
    pallas_call x2, Pallas kernels: 93.6 us -> 91.1 us  [the longest x1 55.8 us: per_device(): call(backward_kernel, f32(8, 2, 4, 32, 256), [HBM], [pltpu.VMEM((32, 2, 3...]
where the time goes in v5:
time: 232 us
  Pallas kernels  227 us (98%)
  local copies, waits for them, and re-layouts  3.65 us (2%)
    pallas_call x1, Pallas kernels, per_device(): call(forward_kernel, (f32(32, 128), f32(8, 256, 128), jax.ShapeDtypeStruc...  136 us
    pallas_call x1, Pallas kernels, per_device(): call(backward_kernel, f32(8, 2, 4, 32, 256), [HBM], [pltpu.VMEM((32, 2, 3...  55.8 us
    pallas_call x1, Pallas kernels, per_device(): call(scatter_kernel, f32(8, 4, 2, 32, 256), [SMEM] + in_vmem(2) + [ANY] *...  35.3 us

profile of v5, /device:TPU:1, one launch (start us, length us, event | category | flops | bytes accessed | tf_op | source)
XLA Modules:
  0.0 231.7 jit_solution(10065934629665719663)
XLA Ops:
  0.6 136.3 %shard_map.131 = (f32[32,128]{1,0:T(8,128)}, f32[8,256,128]{2,1,0:T(8,128)}, s32[32,1,128]{2,1,0:T(1,128)}, s32[32,1,128]{2,1,0:T(1,128)}, f32[2,256,128]{2,1,0:T(8,128)}, /*index=5*/bf16[2,128,512]{2,1,0:T(8,128)(2,1)}) custom-call(s32[16]{0:T(128)} %slot_ref.1, s32[16]{0:T(128)} %bitcast.17, s32[16]{0:T(128)} %plane_ref.1, s32[16]{0:T(128)} %count_ref.1, ...), custom_call_target="tpu_custom_call" | custom-call | tf_op jit(solution)/shard_map/pallas_call | solution.py:740
  137.0 35.3 %shard_map.132 = f32[8,4,2,32,256]{4,3,2,1,0:T(8,128)} custom-call(s32[32,1,128]{2,1,0:T(1,128)} %get-tuple-element.7.idx_ref, f32[2,256,128]{2,1,0:T(8,128)} %get-tuple-element.8.tw_ref, bf16[2,128,512]{2,1,0:T(8,128)(2,1)} %get-tuple-element.9.f_ref, f32[2048,128]{1,0:T(8,128)} %bitcast.13, bf16[4,256,256]{2,1,0:T(8,128)(2,1)} %constant.12.clone.m_any, ...), custom_call_target="tpu_custom_call" | custom-call | tf_op jit(solution)/shard_map/pallas_call | solution.py:809
  172.3 0.0 copy-start
  172.3 1.6 copy-done
  173.9 55.8 %shard_map.133 = f32[8,2,4,32,256]{4,3,2,1,0:T(8,128)S(1)} custom-call(f32[32,2,32,256]{3,2,1,0:T(8,128)S(1)} %bitcast.10), custom_call_target="tpu_custom_call" | custom-call | tf_op jit(solution)/shard_map/pallas_call | solution.py:827
  229.6 0.0 copy-start.1
  229.7 1.5 copy.14
  231.1 0.0 copy-done.1
  231.1 0.6 copy.16
Async XLA Ops:
  172.3 1.6 copy-start
  229.6 1.5 copy-start.1
